TPU v7x, 256 devices: a whole 4x4x8 slice. The times are simulated.
256 devices in a mesh: group: 2 (over core), gx: 16 (over y, x), gy: 8 (over z).
Axes of the slice: x: 4, y: 4, z: 8, core: 2. Of those that a mesh axis runs over, the one named last changes fastest.
Arguments:
- forcing: float32 [2, 80, 128, 2048], P('group', None, 'gx', 'gy'), may hold values from -24 to 24
- conduct: bfloat16 [2, 80, 128, 2048], P('group', None, 'gx', 'gy'), may hold values from 0.25 to 4
- diag_add: bfloat16 [2, 80, 128, 2048], P('group', None, 'gx', 'gy'), may hold values from 0.049804688 to 0.5
- ice_mask: int32 [128, 2048], P('gx', 'gy'), may hold values 0 or 1
- grounded: int32 [128, 2048], P('gx', 'gy'), may hold values 0 or 1
Outputs:
- solution: float32 [2, 80, 128, 2048], P('group', None, 'gx', 'gy')
- residual: float32 [2, 80, 128, 2048], P('group', None, 'gx', 'gy')
All inputs are finite; a program needn't handle non-finite values. No bound on the sum of `ice_mask` or of `grounded` on one device may be relied on, other than what follows from the above.
Results may differ from a plain program's by a relative error of at most 0.0003.
Values sent between devices are 32-bit elements; how exact they have to be, the bound alone decides.
A program may use at most 64 MiB of HBM per device.

v0:
```python
import functools

import jax
import jax.numpy as jnp
from jax import lax
from jax.experimental import pallas as pl
from jax.experimental.pallas import tpu as pltpu
from jax.sharding import PartitionSpec as P

ITERS = 6
FIELDS = ITERS + 1
LAYERS = 80
ROWS = 8
SUB = 8
LANES = 128
TILES = 2
CHUNKS = LAYERS // SUB
MESH = pl.DeviceIdType.MESH
F32 = jnp.float32

far_weight = 0.25
cross_weight = 0.5
vertical_weight = 4.0
friction_gain = 8.0

STEPS = ((-1, 0), (1, 0), (0, -1), (0, 1), (-1, -1), (-1, 1), (1, -1), (1, 1))


def roll(value, shift, axis=None):
    return pltpu.roll(value, shift % value.shape[-1 if axis is None else axis],
                      value.ndim - 1 if axis is None else axis)


def unskew(value, step, sub):
    for bit in (1, 2, 4):
        value = jnp.where((sub & bit) != 0, roll(value, -step * bit), value)
    return value


def kernel(
    nx, nz,
    forcing, conduct, diag_add, ice_mask, grounded, out_x, out_r,
    cbf, dbf, ice_v, ground_v, active_v, fs, cn, dn,
    wbuf, hx, hz, hc, pz, pc, ebuf, hbuf, icbuf, gbuf, hwbuf, acc,
    shared_out, shared_in, ar_own, ar_x, ar_own2, ar_z, xs, rs,
    in_sem, out_sem, send_sem, recv_sem, share_sem, ar_sem,
):
    g = lax.axis_index("group")
    x = lax.axis_index("gx")
    z = lax.axis_index("gy")

    lane2 = lax.broadcasted_iota(jnp.int32, (SUB, LANES), 1)
    sub2 = lax.broadcasted_iota(jnp.int32, (SUB, LANES), 0)
    lane3 = lax.broadcasted_iota(jnp.int32, (ROWS, SUB, LANES), 2)
    sub3 = lax.broadcasted_iota(jnp.int32, (ROWS, SUB, LANES), 1)
    lane1 = lax.broadcasted_iota(jnp.int32, (1, LANES), 1)

    def exists(d):
        dx, dz = STEPS[d]
        conds = []
        if dx < 0:
            conds.append(x > 0)
        if dx > 0:
            conds.append(x < nx - 1)
        if dz < 0:
            conds.append(z > 0)
        if dz > 0:
            conds.append(z < nz - 1)
        return functools.reduce(jnp.logical_and, conds)

    def at(d):
        dx, dz = STEPS[d]
        return (g, x + dx, z + dz)

    loads = [
        pltpu.make_async_copy(conduct, cbf, in_sem.at[0]),
        pltpu.make_async_copy(ice_mask, ice_v, in_sem.at[1]),
        pltpu.make_async_copy(grounded, ground_v, in_sem.at[2]),
        pltpu.make_async_copy(forcing.at[:, pl.ds(0, LANES)], fs.at[0], in_sem.at[3]),
        pltpu.make_async_copy(forcing.at[:, pl.ds(LANES, LANES)], fs.at[1], in_sem.at[4]),
        pltpu.make_async_copy(diag_add, dbf, in_sem.at[5]),
    ]
    for load in loads:
        load.start()

    def zero_rims(d):
        @pl.when(jnp.logical_not(exists(d)))
        def _():
            def body(e, carry):
                if d < 2:
                    for j in range(CHUNKS):
                        hx[e, j, d] = jnp.zeros((2, TILES, SUB, LANES), F32)
                elif d < 4:
                    hz[e, :, d - 2] = jnp.zeros((CHUNKS, SUB, LANES), F32)
                else:
                    hc[e, :, d - 4] = jnp.zeros((CHUNKS, 1, LANES), F32)
                return carry
            lax.fori_loop(0, FIELDS, body, 0)

    for d in range(8):
        zero_rims(d)

    barrier = pltpu.get_barrier_semaphore()

    def greet_x(i, carry):
        @pl.when(i != x)
        def _():
            pl.semaphore_signal(barrier, inc=1, device_id=(g, i, z), device_id_type=MESH)
        return carry

    def greet_z(i, carry):
        @pl.when(i != z)
        def _():
            pl.semaphore_signal(barrier, inc=1, device_id=(g, x, i), device_id_type=MESH)
        return carry

    lax.fori_loop(0, nx, greet_x, 0)
    lax.fori_loop(0, nz, greet_z, 0)
    pl.semaphore_signal(barrier, inc=1, device_id=(1 - g, x, z), device_id_type=MESH)
    for d in range(4, 8):
        @pl.when(exists(d))
        def _(d=d):
            pl.semaphore_signal(barrier, inc=1, device_id=at(d), device_id_type=MESH)

    acc[...] = jnp.zeros_like(acc)

    loads[0].wait()
    loads[1].wait()
    loads[2].wait()
    is_ice = jnp.where(g == 0, 1.0, 0.0).astype(F32)
    ice = ice_v[...].astype(F32)
    ground = ground_v[...].astype(F32)
    active_v[...] = ice * (1.0 - (1.0 - is_ice) * ground)

    def couple(i, carry):
        part = pl.ds(pl.multiple_of(i * SUB * ROWS, SUB * ROWS), SUB * ROWS)
        for t in range(TILES):
            columns = slice(t * LANES, (t + 1) * LANES)
            value = jnp.sqrt(cbf[part, columns].astype(F32)).reshape(SUB, ROWS, LANES)
            cn[t, part] = (value * active_v[:, columns][None]).reshape(SUB * ROWS, LANES)
        return carry

    lax.fori_loop(0, CHUNKS, couple, 0)

    beside_x = (x > 0).astype(jnp.int32) + (x < nx - 1).astype(jnp.int32)
    beside_z = (z > 0).astype(jnp.int32) + (z < nz - 1).astype(jnp.int32)
    pl.semaphore_wait(barrier, nx + nz - 1 + beside_x * beside_z)

    def pick(ref, j, t):
        return jnp.stack([ref[t, pl.ds(j * ROWS + r, SUB, stride=CHUNKS * ROWS), :] for r in range(ROWS)])

    def put(ref, j, t, value):
        for r in range(ROWS):
            ref[t, pl.ds(j * ROWS + r, SUB, stride=CHUNKS * ROWS), :] = value[r]

    def copies(e, j, d):
        if d == 0:
            src, dst = wbuf.at[e, j + 1, pl.ds(0, 2)], hx.at[e, j, 1]
        elif d == 1:
            src, dst = wbuf.at[e, j + 1, pl.ds(ROWS - 2, 2)], hx.at[e, j, 0]
        elif d < 4:
            src, dst = pz.at[e, j], hz.at[e, j, 3 - d]
        else:
            src, dst = pc.at[e, j], hc.at[e, j, 7 - d]
        opposite = (1, 0, 3, 2, 7, 6, 5, 4)[d]
        return pltpu.make_async_remote_copy(
            src_ref=src, dst_ref=dst, send_sem=send_sem.at[d],
            recv_sem=recv_sem.at[e, j, opposite], device_id=at(d), device_id_type=MESH)

    def store_field(e, j, parts):
        for t in range(TILES):
            wbuf[e, j + 1, :, t] = parts[t]

        @pl.when(j == 0)
        def _():
            for t in range(TILES):
                wbuf[e, CHUNKS + 1, :, t] = jnp.where(sub3 < SUB - 1, roll(parts[t], SUB - 1, 1), 0.0)

        @pl.when(j == CHUNKS - 1)
        def _():
            for t in range(TILES):
                wbuf[e, 0, :, t] = jnp.where(sub3 > 0, roll(parts[t], 1, 1), 0.0)

    def send_field(e, j, parts):
        rims = jnp.where(lane3 < 2, parts[0], jnp.where(lane3 >= LANES - 2, parts[1], 0.0))
        packed = roll(rims[0], 4)
        for r in range(1, ROWS):
            packed = packed + roll(rims[r], 4 * (r + 1))
        pz[e, j] = packed
        corner = (lane2 == 3) | (lane2 == 4) | (lane2 == 31) | (lane2 == 32)
        spreaded = pltpu.roll(jnp.where(corner, packed, 0.0), 0, 1, stride=2, stride_axis=0)
        pc[e, j] = jnp.sum(spreaded, axis=0, keepdims=True)
        for d in range(8):
            @pl.when(exists(d))
            def _(d=d):
                copies(e, j, d).start()

    def await_rims(e, j):
        for d in range(8):
            @pl.when(exists(d))
            def _(d=d):
                opposite = (1, 0, 3, 2, 7, 6, 5, 4)[d]
                copies(e, j, opposite).wait_recv()

    def spread(e, j):
        centre = [wbuf[e, j + 1, :, t] for t in range(TILES)]
        beside, mixed = [], []
        for t in range(TILES):
            wide = jnp.concatenate([hx[e, j, 0, :, t], centre[t], hx[e, j, 1, :, t]], axis=0)
            near = wide[1:9] + wide[3:11]
            far = wide[0:8] + wide[4:12]
            vertical = wbuf[e, j, :, t] + wbuf[e, j + 2, :, t]
            beside.append(near + far_weight * far + vertical_weight * vertical)
            mixed.append(centre[t] + cross_weight * near)
        first, last = lane3 == 0, lane3 == LANES - 1

        def from_left(pair):
            a, b = roll(pair[0], 1), roll(pair[1], 1)
            return [jnp.where(first, 0.0, a), jnp.where(first, a, b)]

        def from_right(pair):
            a, b = roll(pair[0], -1), roll(pair[1], -1)
            return [jnp.where(last, b, a), jnp.where(last, 0.0, b)]

        for shift in (from_left, from_right):
            once = shift(centre)
            twice = shift([mixed[t] + far_weight * once[t] for t in range(TILES)])
            beside = [beside[t] + twice[t] for t in range(TILES)]

        place = lane2 % 4
        rims = jnp.where(place < 2, roll(hz[e, j, 0], 2), roll(hz[e, j, 1], -2))
        crossed = rims + cross_weight * (roll(rims, 4) + roll(rims, -4))
        edge = far_weight * rims + jnp.where(
            place == 0, roll(crossed, -1), jnp.where(place == 3, roll(crossed, 1), 0.0))
        odd = lane1 % 2 == 1
        corners = jnp.where(
            lane1 >= 31,
            jnp.where(odd, hc[e, j, 0], hc[e, j, 1]),
            jnp.where(odd, hc[e, j, 2], hc[e, j, 3]))
        corners = unskew(jnp.broadcast_to(corners, (SUB, LANES)), 2, sub2)
        edge = edge + cross_weight * jnp.where(
            lane2 == 4, roll(corners, -27), jnp.where(
                lane2 == 3, roll(corners, -29), jnp.where(
                    lane2 == 32, roll(corners, 29), jnp.where(
                        lane2 == 31, roll(corners, 27), 0.0))))
        rows = jnp.stack([roll(edge, -4 * (r + 1)) for r in range(ROWS)])
        return [beside[0] + jnp.where(lane3 < 2, rows, 0.0),
                beside[1] + jnp.where(lane3 >= LANES - 2, rows, 0.0)]

    def dots(k, j, parts):
        for t in range(TILES):
            hwbuf[:, t] = hbuf[j, :, t] * parts[t]

        def body(i, carry):
            product = jnp.sum(hwbuf[...] * wbuf[i + 1, j + 1], axis=(0, 1))
            total = acc[k, i] + product
            acc[k, i] = total
            acc[i, k] = total
            return carry

        lax.fori_loop(0, k + 1, body, 0)

    def first(j, carry):
        parts = [pick(cn, j, t) for t in range(TILES)]
        store_field(0, j, parts)
        send_field(0, j, parts)
        return carry

    lax.fori_loop(0, CHUNKS, first, 0)

    loads[3].wait()
    loads[4].wait()
    edge = pl.ds(pl.multiple_of(g * ((LAYERS - 1) * ROWS), ROWS), ROWS)
    for t in range(TILES):
        mean = jnp.sum(fs[t].reshape(LAYERS, ROWS, LANES), axis=0) * (1.0 / LAYERS)
        value = active_v[:, t * LANES:(t + 1) * LANES] * mean
        shared_out[t] = value * cn[t, edge]
    share = pltpu.make_async_remote_copy(
        src_ref=shared_out, dst_ref=shared_in, send_sem=share_sem.at[0], recv_sem=share_sem.at[1],
        device_id=(1 - g, x, z), device_id_type=MESH)
    share.start()
    loads[5].wait()

    def widen(i, carry):
        part = pl.ds(pl.multiple_of(i * SUB * ROWS, SUB * ROWS), SUB * ROWS)
        for t in range(TILES):
            dn[t, part] = dbf[part, t * LANES:(t + 1) * LANES].astype(F32)
        return carry

    lax.fori_loop(0, CHUNKS, widen, 0)
    share.wait()
    for t in range(TILES):
        columns = slice(t * LANES, (t + 1) * LANES)
        friction = is_ice * friction_gain * (ground_v[:, columns].astype(F32) * ice_v[:, columns].astype(F32))
        dn[t, 0:ROWS] = dn[t, 0:ROWS] + friction
        fs[t, edge] = fs[t, edge] + shared_in[t]

    def second(j, carry):
        await_rims(0, j)
        spreads = spread(0, j)
        parts = []
        for t in range(TILES):
            c = wbuf[0, j + 1, :, t]
            diagonal = pick(dn, j, t) + c * spreads[t]
            ratio = c / diagonal
            inverse_c = jnp.where(c > 0.0, 1.0 / jnp.where(c > 0.0, c, 1.0), 0.0)
            back = diagonal * inverse_c
            ebuf[j, :, t] = ratio * c
            icbuf[j, :, t] = inverse_c
            gbuf[j, :, t] = back
            hbuf[j, :, t] = back * inverse_c
            parts.append(ratio * pick(fs, j, t))
        store_field(1, j, parts)
        send_field(1, j, parts)
        dots(0, j, parts)
        return carry

    lax.fori_loop(0, CHUNKS, second, 0)

    def stage(k, carry):
        gain = jnp.where(k == 1, 1.0, 2.0).astype(F32)
        keep = jnp.where(k == 1, 0.0, 1.0).astype(F32)

        def body(j, inner):
            await_rims(k, j)
            spreads = spread(k, j)
            parts = [gain * (ebuf[j, :, t] * spreads[t]) - keep * wbuf[k - 1, j + 1, :, t]
                     for t in range(TILES)]
            store_field(k + 1, j, parts)

            @pl.when(k < ITERS)
            def _():
                send_field(k + 1, j, parts)
            dots(k, j, parts)
            return inner

        return lax.fori_loop(0, CHUNKS, body, carry)

    lax.fori_loop(1, ITERS + 1, stage, 0)

    gram = jnp.zeros((SUB, LANES), F32)
    for k in range(FIELDS):
        column = jnp.sum(jnp.sum(acc[k], axis=1), axis=1, keepdims=True)
        gram = gram + jnp.where(lane2 == k, column, 0.0)
    row = jnp.sum(pltpu.roll(gram, 0, 1, stride=SUB, stride_axis=0), axis=0, keepdims=True)
    ar_own[...] = row

    def scatter(own, slots, count, me, device, sems):
        def one(i, carry):
            @pl.when(i != me)
            def _():
                pltpu.make_async_remote_copy(
                    src_ref=own, dst_ref=slots.at[me], send_sem=sems.at[0], recv_sem=sems.at[1],
                    device_id=device(i), device_id_type=MESH).start()
            return carry
        lax.fori_loop(0, count, one, 0)
        slots[me] = own[...]
        rest = slots.at[pl.ds(0, count - 1)]
        pltpu.make_async_copy(rest, rest, sems.at[1]).wait()
        return jnp.sum(slots[...], axis=0)

    ar_own2[...] = scatter(ar_own, ar_x, nx, x, lambda i: (g, i, z), ar_sem.at[0])
    total = scatter(ar_own2, ar_z, nz, z, lambda i: (g, x, i), ar_sem.at[1])

    gram = unskew(jnp.broadcast_to(total, (SUB, LANES)), SUB, sub2)
    gram = jnp.where((lane2 < FIELDS) & (sub2 < ITERS), gram, 0.0)
    system = gram - jnp.where(lane2 == 0, 1.0, 0.5) * roll(gram, -1) - 0.5 * roll(gram, 1)
    system = jnp.where(lane2 < ITERS, system, jnp.where(lane2 == ITERS, roll(gram, ITERS), 0.0))
    for p in range(ITERS):
        pivot_row = system[p:p + 1, :] / system[p:p + 1, p:p + 1]
        system = jnp.where(sub2 == p, pivot_row, system - system[:, p:p + 1] * pivot_row)
    a = [system[k:k + 1, ITERS:ITERS + 1] for k in range(ITERS)]
    b = [None] * FIELDS
    b[0] = 1.0 - a[0] + 0.5 * a[1]
    b[1] = a[0] - a[1] + 0.5 * a[2]
    for k in range(2, ITERS - 1):
        b[k] = 0.5 * (a[k - 1] + a[k + 1]) - a[k]
    b[ITERS - 1] = 0.5 * a[ITERS - 2] - a[ITERS - 1]
    b[ITERS] = 0.5 * a[ITERS - 1]
    a = [jnp.broadcast_to(v, (SUB, LANES)) for v in a]
    b = [jnp.broadcast_to(v, (SUB, LANES)) for v in b]

    def combine(j, carry):
        for t in range(TILES):
            fields = [wbuf[k + 1, j + 1, :, t] for k in range(FIELDS)]
            up = a[0][None] * fields[0]
            down = b[0][None] * fields[0]
            for k in range(1, ITERS):
                up = up + a[k][None] * fields[k]
                down = down + b[k][None] * fields[k]
            down = down + b[ITERS][None] * fields[ITERS]
            put(xs, j, t, icbuf[j, :, t] * up)
            put(rs, j, t, gbuf[j, :, t] * down)
        return carry

    lax.fori_loop(0, CHUNKS, combine, 0)
    stores = []
    for t in range(TILES):
        lanes = pl.ds(t * LANES, LANES)
        stores.append(pltpu.make_async_copy(xs.at[t], out_x.at[:, lanes], out_sem.at[t]))
        stores.append(pltpu.make_async_copy(rs.at[t], out_r.at[:, lanes], out_sem.at[2 + t]))
    for store in stores:
        store.start()

    for d in range(8):
        @pl.when(exists(d))
        def _(d=d):
            whole = hx.at[:, :, d] if d < 2 else hz.at[:, :, d - 2] if d < 4 else hc.at[:, :, d - 4]
            pltpu.make_async_copy(whole, whole, send_sem.at[d]).wait()
    sent = ar_x.at[pl.ds(0, nx - 1)]
    pltpu.make_async_copy(sent, sent, ar_sem.at[0, 0]).wait()
    sent = ar_z.at[pl.ds(0, nz - 1)]
    pltpu.make_async_copy(sent, sent, ar_sem.at[1, 0]).wait()
    for store in stores:
        store.wait()


def on_device(nx, nz, forcing, conduct, diag_add, ice_mask, grounded):
    field = (CHUNKS, ROWS, TILES, SUB, LANES)
    native = (TILES, LAYERS * ROWS, LANES)
    wide = TILES * LANES
    any_space = pl.BlockSpec(memory_space=pl.ANY)
    out = jax.ShapeDtypeStruct((LAYERS * ROWS, wide), F32)
    vmem = pltpu.VMEM
    flat = lambda array: array.reshape(LAYERS * ROWS, wide)
    outs = pl.pallas_call(
        functools.partial(kernel, nx, nz),
        out_shape=(out, out),
        in_specs=[any_space] * 5,
        out_specs=(any_space, any_space),
        scratch_shapes=[
            vmem((LAYERS * ROWS, wide), jnp.bfloat16),
            vmem((LAYERS * ROWS, wide), jnp.bfloat16),
            vmem((ROWS, wide), jnp.int32),
            vmem((ROWS, wide), jnp.int32),
            vmem((ROWS, wide), F32),
            vmem(native, F32),
            vmem(native, F32),
            vmem(native, F32),
            vmem((FIELDS + 1, CHUNKS + 2, ROWS, TILES, SUB, LANES), F32),
            vmem((FIELDS, CHUNKS, 2, 2, TILES, SUB, LANES), F32),
            vmem((FIELDS, CHUNKS, 2, SUB, LANES), F32),
            vmem((FIELDS, CHUNKS, 4, 1, LANES), F32),
            vmem((FIELDS, CHUNKS, SUB, LANES), F32),
            vmem((FIELDS, CHUNKS, 1, LANES), F32),
            vmem(field, F32),
            vmem(field, F32),
            vmem(field, F32),
            vmem(field, F32),
            vmem((ROWS, TILES, SUB, LANES), F32),
            vmem((SUB, SUB, SUB, LANES), F32),
            vmem((TILES, ROWS, LANES), F32),
            vmem((TILES, ROWS, LANES), F32),
            vmem((1, LANES), F32),
            vmem((nx, 1, LANES), F32),
            vmem((1, LANES), F32),
            vmem((nz, 1, LANES), F32),
            vmem(native, F32),
            vmem(native, F32),
            pltpu.SemaphoreType.DMA((6,)),
            pltpu.SemaphoreType.DMA((4,)),
            pltpu.SemaphoreType.DMA((8,)),
            pltpu.SemaphoreType.DMA((FIELDS, CHUNKS, 8)),
            pltpu.SemaphoreType.DMA((2,)),
            pltpu.SemaphoreType.DMA((2, 2)),
        ],
        compiler_params=pltpu.CompilerParams(collective_id=0, has_side_effects=True),
        name="coupled_solve",
    )(flat(forcing), flat(conduct), flat(diag_add), ice_mask, grounded)
    return tuple(v.reshape(1, LAYERS, ROWS, wide) for v in outs)


def solution(mesh):
    block = P("group", None, "gx", "gy")
    columns = P("gx", "gy")
    return jax.shard_map(
        functools.partial(on_device, mesh.shape["gx"], mesh.shape["gy"]),
        mesh=mesh,
        in_specs=(block, block, block, columns, columns),
        out_specs=(block, block),
        check_vma=False,
    )
```

profile of v0, /device:TPU:2, one launch (start us, length us, event | category | flops | bytes accessed | tf_op | source)
XLA Modules:
  0.0 79.8 jit_solution(2787528205020441965)
XLA Ops:
  0.6 76.2 %coupled_solve.1 = (f32[640,256]{1,0:T(8,128)}, f32[640,256]{1,0:T(8,128)}) custom-call(f32[640,256]{1,0:T(8,128)} %bitcast.7, bf16[640,256]{1,0:T(8,128)(2,1)} %bitcast.8, bf16[640,256]{1,0:T(8,128)(2,1)} %bitcast.9, s32[8,256]{1,0:T(8,128)} %ice_mask.1, s32[8,256]{1,0:T(8,128)} %grounded.1), custom_call_target="tpu_custom_call" | custom-call | tf_op jit(solution)/shard_map/coupled_solve/pallas_call | solution.py:426
  76.9 0.0 copy-start
  76.9 2.0 %copy.9 = f32[1,80,8,256]{3,2,1,0:T(8,128)} copy(f32[1,80,8,256]{3,2,1,0:T(8,128)} %bitcast.6) | data formatting | bytes 1310720
  78.9 0.0 copy-done
  78.9 0.8 %copy.10 = f32[1,80,8,256]{3,2,1,0:T(8,128)} copy(f32[1,80,8,256]{3,2,1,0:T(8,128)S(1)} %bitcast.5) | data formatting | bytes 1310720
Async XLA Ops:
  76.9 2.0 %copy-start = (f32[640,256]{1,0:T(8,128)S(1)}, f32[640,256]{1,0:T(8,128)}, u32[]{:S(2)}) copy-start(f32[640,256]{1,0:T(8,128)} %get-tuple-element.5) | copy-start | bytes 1966084
where the time goes:
time: 79.9 us; the launch traced here: 79.8 us
  Pallas kernels  76.2 us (95%)
  local copies, waits for them, and re-layouts  2.87 us (4%)
    pallas_call x1, Pallas kernels, on_device(): pl.pallas_call(functools.partial(kernel, nx, nz), out_shape=(out, out), i...  76.2 us
    unnamed x4, local copies, waits for them, and re-layouts  2.87 us

commit v1 on v0

v1 whole, which is shorter than its diff:
```python
import functools

import jax
import jax.numpy as jnp
from jax import lax
from jax.experimental import pallas as pl
from jax.experimental.pallas import tpu as pltpu
from jax.sharding import PartitionSpec as P

ITERS = 6
FIELDS = ITERS + 1
COUPLING = FIELDS + 1
LAYERS = 80
ROWS = 8
SUB = 8
LANES = 128
TILES = 2
CHUNKS = LAYERS // SUB
MESH = pl.DeviceIdType.MESH
F32 = jnp.float32

far_weight = 0.25
cross_weight = 0.5
vertical_weight = 4.0
friction_gain = 8.0

STEPS = ((-1, 0), (1, 0), (0, -1), (0, 1), (-1, -1), (-1, 1), (1, -1), (1, 1))


def roll(value, shift, axis=None):
    return pltpu.roll(value, shift % value.shape[-1 if axis is None else axis],
                      value.ndim - 1 if axis is None else axis)


def far_first(count):
    return sorted(range(1, count), key=lambda i: -min(i, count - i))


def kernel(
    nx, nz,
    forcing, conduct, diag_add, ice_mask, grounded, out_x, out_r,
    cbf, dbf, ice_v, ground_v, active_v, fs, cn, dn,
    wbuf, hx, hz, hc, pz, pc, ebuf, hbuf, icbuf, gbuf, acc,
    shared_out, shared_in, ar_own, ar_x, ar_own2, ar_z,
    in_sem, send_sem, recv_sem, share_sem, ar_sem,
):
    g = lax.axis_index("group")
    x = lax.axis_index("gx")
    z = lax.axis_index("gy")

    lane2 = lax.broadcasted_iota(jnp.int32, (SUB, LANES), 1)
    sub2 = lax.broadcasted_iota(jnp.int32, (SUB, LANES), 0)
    lane3 = lax.broadcasted_iota(jnp.int32, (ROWS, SUB, LANES), 2)
    sub3 = lax.broadcasted_iota(jnp.int32, (ROWS, SUB, LANES), 1)
    lane1 = lax.broadcasted_iota(jnp.int32, (1, LANES), 1)

    def exists(d):
        dx, dz = STEPS[d]
        conds = []
        if dx < 0:
            conds.append(x > 0)
        if dx > 0:
            conds.append(x < nx - 1)
        if dz < 0:
            conds.append(z > 0)
        if dz > 0:
            conds.append(z < nz - 1)
        return functools.reduce(jnp.logical_and, conds)

    def at(d):
        dx, dz = STEPS[d]
        return (g, x + dx, z + dz)

    loads = [
        pltpu.make_async_copy(conduct, cbf, in_sem.at[0]),
        pltpu.make_async_copy(ice_mask, ice_v, in_sem.at[1]),
        pltpu.make_async_copy(grounded, ground_v, in_sem.at[2]),
        pltpu.make_async_copy(forcing.at[:, pl.ds(0, LANES)], fs.at[0], in_sem.at[3]),
        pltpu.make_async_copy(forcing.at[:, pl.ds(LANES, LANES)], fs.at[1], in_sem.at[4]),
        pltpu.make_async_copy(diag_add, dbf, in_sem.at[5]),
    ]
    for load in loads:
        load.start()

    def zero_rims(d):
        @pl.when(jnp.logical_not(exists(d)))
        def _():
            def body(e, carry):
                if d < 2:
                    for j in range(CHUNKS):
                        hx[e, j, d] = jnp.zeros((2, TILES, SUB, LANES), F32)
                elif d < 4:
                    hz[e, :, d - 2] = jnp.zeros((CHUNKS, SUB, LANES), F32)
                else:
                    hc[e, :, d - 4] = jnp.zeros((CHUNKS, 1, LANES), F32)
                return carry
            lax.fori_loop(0, FIELDS, body, 0)

    for d in range(8):
        zero_rims(d)

    barrier = pltpu.get_barrier_semaphore()

    def greet_x(i, carry):
        @pl.when(i != x)
        def _():
            pl.semaphore_signal(barrier, inc=1, device_id=(g, i, z), device_id_type=MESH)
        return carry

    def greet_z(i, carry):
        @pl.when(i != z)
        def _():
            pl.semaphore_signal(barrier, inc=1, device_id=(g, x, i), device_id_type=MESH)
        return carry

    lax.fori_loop(0, nx, greet_x, 0)
    lax.fori_loop(0, nz, greet_z, 0)
    pl.semaphore_signal(barrier, inc=1, device_id=(1 - g, x, z), device_id_type=MESH)
    for d in range(4, 8):
        @pl.when(exists(d))
        def _(d=d):
            pl.semaphore_signal(barrier, inc=1, device_id=at(d), device_id_type=MESH)

    acc[...] = jnp.zeros_like(acc)

    def clear(f, carry):
        for j in range(CHUNKS):
            wbuf[f, j + 1] = jnp.zeros((ROWS, TILES, SUB, LANES), F32)
        return carry

    lax.fori_loop(0, FIELDS + 1, clear, 0)

    loads[0].wait()
    loads[1].wait()
    loads[2].wait()
    is_ice = jnp.where(g == 0, 1.0, 0.0).astype(F32)
    ice = ice_v[...].astype(F32)
    ground = ground_v[...].astype(F32)
    active_v[...] = ice * (1.0 - (1.0 - is_ice) * ground)

    def couple(i, carry):
        part = pl.ds(pl.multiple_of(i * SUB * ROWS, SUB * ROWS), SUB * ROWS)
        for t in range(TILES):
            columns = slice(t * LANES, (t + 1) * LANES)
            value = jnp.sqrt(cbf[part, columns].astype(F32)).reshape(SUB, ROWS, LANES)
            cn[t, part] = (value * active_v[:, columns][None]).reshape(SUB * ROWS, LANES)
        return carry

    lax.fori_loop(0, CHUNKS, couple, 0)


    def pick(ref, j, t):
        return jnp.stack([ref[t, pl.ds(j * ROWS + r, SUB, stride=CHUNKS * ROWS), :] for r in range(ROWS)])

    def put(ref, j, t, value):
        for r in range(ROWS):
            ref[t, pl.ds(j * ROWS + r, SUB, stride=CHUNKS * ROWS), :] = value[r]

    def copies(e, j, d):
        f = COUPLING if isinstance(e, int) and e == 0 else e
        if d == 0:
            src, dst = wbuf.at[f, j + 1, pl.ds(0, 2)], hx.at[e, j, 1]
        elif d == 1:
            src, dst = wbuf.at[f, j + 1, pl.ds(ROWS - 2, 2)], hx.at[e, j, 0]
        elif d < 4:
            src, dst = pz.at[e, j], hz.at[e, j, 3 - d]
        else:
            src, dst = pc.at[e, j], hc.at[e, j, 7 - d]
        opposite = (1, 0, 3, 2, 7, 6, 5, 4)[d]
        return pltpu.make_async_remote_copy(
            src_ref=src, dst_ref=dst, send_sem=send_sem.at[d],
            recv_sem=recv_sem.at[e, j, opposite], device_id=at(d), device_id_type=MESH)

    def store_field(f, j, parts):
        for t in range(TILES):
            wbuf[f, j + 1, :, t] = parts[t]

        @pl.when(j == 0)
        def _():
            for t in range(TILES):
                wbuf[f, CHUNKS + 1, :, t] = jnp.where(sub3 < SUB - 1, roll(parts[t], SUB - 1, 1), 0.0)

        @pl.when(j == CHUNKS - 1)
        def _():
            for t in range(TILES):
                wbuf[f, 0, :, t] = jnp.where(sub3 > 0, roll(parts[t], 1, 1), 0.0)

    def pack_rims(e, j, parts):
        none = jnp.zeros((1, SUB, LANES), F32)
        crossed, scaled = [], []
        for t in range(TILES):
            wide = jnp.concatenate([none, parts[t], none], axis=0)
            crossed.append(parts[t] + cross_weight * (wide[0:8] + wide[2:10]))
            scaled.append(far_weight * parts[t])
        sources = (
            (jnp.where(lane3 == LANES - 1, crossed[1], 0.0), 1),
            (jnp.where(lane3 == 0, crossed[0], 0.0), -1),
            (jnp.where(lane3 >= LANES - 2, scaled[1], 0.0), 2),
            (jnp.where(lane3 < 2, scaled[0], 0.0), -2),
        )
        packed = None
        for source, shift in sources:
            for r in range(ROWS):
                moved = roll(source[r], 4 * (r + 1) + shift)
                packed = moved if packed is None else packed + moved
        pz[e, j] = packed
        corners = None
        for q in range(4):
            row, tile = (0, ROWS - 1)[q // 2], q % 2
            lane = (0, LANES - 1)[tile]
            only = jnp.where(lane2 == lane, cross_weight * parts[tile][row], 0.0)
            moved = pltpu.roll(only, (8 * q - lane) % LANES, 1, stride=1, stride_axis=0)
            corners = moved if corners is None else corners + moved
        pc[e, j] = jnp.sum(corners, axis=0, keepdims=True)

    def send_rims(e, j, wanted):
        for d in range(8):
            @pl.when(exists(d) if wanted is None else jnp.logical_and(exists(d), wanted))
            def _(d=d):
                copies(e, j, d).start()

    def await_rims(e, j):
        for d in range(8):
            @pl.when(exists(d))
            def _(d=d):
                opposite = (1, 0, 3, 2, 7, 6, 5, 4)[d]
                copies(e, j, opposite).wait_recv()

    def spread(f, e, j):
        centre = [wbuf[f, j + 1, :, t] for t in range(TILES)]
        beside, mixed, scaled = [], [], []
        for t in range(TILES):
            wide = jnp.concatenate([hx[e, j, 0, :, t], centre[t], hx[e, j, 1, :, t]], axis=0)
            near = wide[1:9] + wide[3:11]
            far = wide[0:8] + wide[4:12]
            vertical = wbuf[f, j, :, t] + wbuf[f, j + 2, :, t]
            beside.append(near + far_weight * far + vertical_weight * vertical)
            mixed.append(centre[t] + cross_weight * near)
            scaled.append(far_weight * centre[t])
        for source, shift in ((mixed, 1), (scaled, 2)):
            a, b = roll(source[0], shift), roll(source[1], shift)
            beside[0] = beside[0] + jnp.where(lane3 < shift, 0.0, a)
            beside[1] = beside[1] + jnp.where(lane3 < shift, a, b)
            a, b = roll(source[0], -shift), roll(source[1], -shift)
            beside[0] = beside[0] + jnp.where(lane3 >= LANES - shift, b, a)
            beside[1] = beside[1] + jnp.where(lane3 >= LANES - shift, 0.0, b)

        edge = jnp.where(lane2 % 4 < 2, hz[e, j, 0], hz[e, j, 1])
        rows = [roll(edge, -4 * (r + 1)) for r in range(ROWS)]
        corner = []
        for q in range(4):
            picked = jnp.where(lane2 == 8 * (3 - q) + sub2, jnp.broadcast_to(hc[e, j, q], (SUB, LANES)), 0.0)
            corner.append(jnp.sum(picked, axis=1, keepdims=True))
        rows[0] = rows[0] + jnp.where(lane2 == 0, corner[0], jnp.where(lane2 == LANES - 1, corner[1], 0.0))
        rows[-1] = rows[-1] + jnp.where(lane2 == 0, corner[2], jnp.where(lane2 == LANES - 1, corner[3], 0.0))
        rows = jnp.stack(rows)
        return [beside[0] + jnp.where(lane3 < 2, rows, 0.0),
                beside[1] + jnp.where(lane3 >= LANES - 2, rows, 0.0)]

    def dots(k, j, parts, count):
        weighted = [hbuf[j, :, t] * parts[t] for t in range(TILES)]
        for i in range(count):
            product = [jnp.sum(weighted[t] * wbuf[i + 1, j + 1, :, t], axis=0) for t in range(TILES)]
            acc[k, i] = acc[k, i] + (product[0] + product[1])

    beside_x = (x > 0).astype(jnp.int32) + (x < nx - 1).astype(jnp.int32)
    beside_z = (z > 0).astype(jnp.int32) + (z < nz - 1).astype(jnp.int32)
    pl.semaphore_wait(barrier, nx + nz - 1 + beside_x * beside_z)
    def first(j, carry):
        parts = [pick(cn, j, t) for t in range(TILES)]
        store_field(COUPLING, j, parts)
        pack_rims(0, j, parts)
        send_rims(0, j, None)
        return carry

    lax.fori_loop(0, CHUNKS, first, 0)

    loads[3].wait()
    loads[4].wait()
    edge = pl.ds(pl.multiple_of(g * ((LAYERS - 1) * ROWS), ROWS), ROWS)
    for t in range(TILES):
        mean = jnp.sum(fs[t].reshape(LAYERS, ROWS, LANES), axis=0) * (1.0 / LAYERS)
        value = active_v[:, t * LANES:(t + 1) * LANES] * mean
        shared_out[t] = value * cn[t, edge]
    loads[5].wait()

    def widen(i, carry):
        part = pl.ds(pl.multiple_of(i * SUB * ROWS, SUB * ROWS), SUB * ROWS)
        for t in range(TILES):
            dn[t, part] = dbf[part, t * LANES:(t + 1) * LANES].astype(F32)
        return carry

    lax.fori_loop(0, CHUNKS, widen, 0)
    for t in range(TILES):
        columns = slice(t * LANES, (t + 1) * LANES)
        friction = is_ice * friction_gain * (ground_v[:, columns].astype(F32) * ice_v[:, columns].astype(F32))
        dn[t, 0:ROWS] = dn[t, 0:ROWS] + friction

    share = pltpu.make_async_remote_copy(
        src_ref=shared_out, dst_ref=shared_in, send_sem=share_sem.at[0], recv_sem=share_sem.at[1],
        device_id=(1 - g, x, z), device_id_type=MESH)
    share.start()

    share.wait()
    for t in range(TILES):
        fs[t, edge] = fs[t, edge] + shared_in[t]

    def second(j, carry):
        await_rims(0, j)
        spreads = spread(COUPLING, 0, j)
        parts = []
        for t in range(TILES):
            c = wbuf[COUPLING, j + 1, :, t]
            diagonal = pick(dn, j, t) + c * spreads[t]
            ratio = c / diagonal
            inverse_c = jnp.where(c > 0.0, 1.0 / jnp.where(c > 0.0, c, 1.0), 0.0)
            back = diagonal * inverse_c
            ebuf[j, :, t] = 2.0 * ratio * c
            icbuf[j, :, t] = inverse_c
            gbuf[j, :, t] = back
            hbuf[j, :, t] = back * inverse_c
            parts.append(ratio * pick(fs, j, t))
        store_field(1, j, parts)
        pack_rims(1, j, parts)
        dots(0, j, parts, 1)
        send_rims(1, j, None)
        return carry

    lax.fori_loop(0, CHUNKS, second, 0)

    def stage(k, carry):
        def body(j, inner):
            await_rims(k, j)
            spreads = spread(k, k, j)
            parts = [ebuf[j, :, t] * spreads[t] - wbuf[k - 1, j + 1, :, t] for t in range(TILES)]
            store_field(k + 1, j, parts)
            pack_rims(k + 1, j, parts)
            dots(k, j, parts, FIELDS)
            send_rims(k + 1, j, k < ITERS)
            return inner

        return lax.fori_loop(0, CHUNKS, body, carry)

    lax.fori_loop(1, ITERS + 1, stage, 0)

    gram = jnp.zeros((SUB, LANES), F32)
    for k in range(FIELDS):
        column = jnp.sum(jnp.sum(acc[k], axis=1), axis=1, keepdims=True)
        gram = gram + jnp.where((lane2 == SUB * sub2 + k) & (sub2 <= k), column, 0.0)
    row = jnp.sum(gram, axis=0, keepdims=True)
    ar_own[...] = row

    def scatter(own, slots, me, count, offsets, device, sems):
        for offset in offsets:
            pltpu.make_async_remote_copy(
                src_ref=own, dst_ref=slots.at[me], send_sem=sems.at[0], recv_sem=sems.at[1],
                device_id=device((me + offset) % count), device_id_type=MESH).start()
        slots[me] = own[...]
        rest = slots.at[pl.ds(0, count - 1)]
        pltpu.make_async_copy(rest, rest, sems.at[1]).wait()
        return jnp.sum(slots[...], axis=0)

    ar_own2[...] = scatter(ar_own, ar_x, x, nx, far_first(nx), lambda i: (g, i, z), ar_sem.at[0])
    total = scatter(ar_own2, ar_z, z, nz, far_first(nz), lambda i: (g, x, i), ar_sem.at[1])

    total = jnp.broadcast_to(total, (SUB, LANES))

    def entry(i, k):
        lane = SUB * min(i, k) + max(i, k)
        return jnp.broadcast_to(total[:, lane:lane + 1], (SUB, LANES))

    gram = [[entry(i, k) for k in range(i, FIELDS)] for i in range(ITERS)]
    inner = lambda i, k: gram[min(i, k)][abs(i - k)]
    system = {(i, k): inner(i, k) - 0.5 * (inner(i, k + 1) + inner(i, k - 1) if k else inner(i, 1))
              for i in range(ITERS) for k in range(i, ITERS)}
    right = [inner(0, i) for i in range(ITERS)]
    inverse = []
    for p in range(ITERS):
        inverse.append(1.0 / system[p, p])
        for i in range(p + 1, ITERS):
            factor = system[p, i] * inverse[p]
            for k in range(i, ITERS):
                system[i, k] = system[i, k] - factor * system[p, k]
            right[i] = right[i] - factor * right[p]
    a = [None] * ITERS
    for p in reversed(range(ITERS)):
        value = right[p]
        for k in range(p + 1, ITERS):
            value = value - system[p, k] * a[k]
        a[p] = value * inverse[p]
    b = [None] * FIELDS
    b[0] = 1.0 - a[0] + 0.5 * a[1]
    for k in range(1, ITERS - 1):
        b[k] = 0.5 * (a[k - 1] + a[k + 1]) - a[k]
    b[ITERS - 1] = 0.5 * a[ITERS - 2] - a[ITERS - 1]
    b[ITERS] = 0.5 * a[ITERS - 1]
    def combine(j, carry):
        for t in range(TILES):
            fields = [wbuf[k + 1, j + 1, :, t] for k in range(FIELDS)]
            up = a[0][None] * fields[0]
            down = b[0][None] * fields[0]
            for k in range(1, ITERS):
                up = up + a[k][None] * fields[k]
                down = down + b[k][None] * fields[k]
            down = down + b[ITERS][None] * fields[ITERS]
            put(out_x, j, t, icbuf[j, :, t] * up)
            put(out_r, j, t, gbuf[j, :, t] * down)
        return carry

    lax.fori_loop(0, CHUNKS, combine, 0)
    for d in range(8):
        @pl.when(exists(d))
        def _(d=d):
            whole = hx.at[:, :, d] if d < 2 else hz.at[:, :, d - 2] if d < 4 else hc.at[:, :, d - 4]
            pltpu.make_async_copy(whole, whole, send_sem.at[d]).wait()
    sent = ar_x.at[pl.ds(0, nx - 1)]
    pltpu.make_async_copy(sent, sent, ar_sem.at[0, 0]).wait()
    sent = ar_z.at[pl.ds(0, nz - 1)]
    pltpu.make_async_copy(sent, sent, ar_sem.at[1, 0]).wait()


def on_device(nx, nz, forcing, conduct, diag_add, ice_mask, grounded):
    field = (CHUNKS, ROWS, TILES, SUB, LANES)
    native = (TILES, LAYERS * ROWS, LANES)
    wide = TILES * LANES
    hbm_space = pl.BlockSpec(memory_space=pltpu.HBM)
    vmem_space = pl.BlockSpec(memory_space=pltpu.VMEM)
    out = jax.ShapeDtypeStruct(native, F32)
    vmem = pltpu.VMEM
    flat = lambda array: array.reshape(LAYERS * ROWS, wide)
    outs = pl.pallas_call(
        functools.partial(kernel, nx, nz),
        out_shape=(out, out),
        in_specs=[hbm_space] * 5,
        out_specs=(vmem_space, vmem_space),
        scratch_shapes=[
            vmem((LAYERS * ROWS, wide), jnp.bfloat16),
            vmem((LAYERS * ROWS, wide), jnp.bfloat16),
            vmem((ROWS, wide), jnp.int32),
            vmem((ROWS, wide), jnp.int32),
            vmem((ROWS, wide), F32),
            vmem(native, F32),
            vmem(native, F32),
            vmem(native, F32),
            vmem((COUPLING + 1, CHUNKS + 2, ROWS, TILES, SUB, LANES), F32),
            vmem((FIELDS, CHUNKS, 2, 2, TILES, SUB, LANES), F32),
            vmem((FIELDS, CHUNKS, 2, SUB, LANES), F32),
            vmem((FIELDS, CHUNKS, 4, 1, LANES), F32),
            vmem((FIELDS + 1, CHUNKS, SUB, LANES), F32),
            vmem((FIELDS + 1, CHUNKS, 1, LANES), F32),
            vmem(field, F32),
            vmem(field, F32),
            vmem(field, F32),
            vmem(field, F32),
            vmem((SUB, SUB, SUB, LANES), F32),
            vmem((TILES, ROWS, LANES), F32),
            vmem((TILES, ROWS, LANES), F32),
            vmem((1, LANES), F32),
            vmem((nx, 1, LANES), F32),
            vmem((1, LANES), F32),
            vmem((nz, 1, LANES), F32),
            pltpu.SemaphoreType.DMA((6,)),
            pltpu.SemaphoreType.DMA((8,)),
            pltpu.SemaphoreType.DMA((FIELDS, CHUNKS, 8)),
            pltpu.SemaphoreType.DMA((2,)),
            pltpu.SemaphoreType.DMA((2, 2)),
        ],
        compiler_params=pltpu.CompilerParams(collective_id=0, has_side_effects=True, vmem_limit_bytes=40 * 1024 * 1024),
        name="coupled_solve",
    )(*[pltpu.with_memory_space_constraint(v, pltpu.HBM)
        for v in (flat(forcing), flat(conduct), flat(diag_add), ice_mask, grounded)])
    return tuple(
        v.reshape(TILES, LAYERS, ROWS, LANES).transpose(1, 2, 0, 3).reshape(1, LAYERS, ROWS, wide)
        for v in outs)


def solution(mesh):
    block = P("group", None, "gx", "gy")
    columns = P("gx", "gy")
    return jax.shard_map(
        functools.partial(on_device, mesh.shape["gx"], mesh.shape["gy"]),
        mesh=mesh,
        in_specs=(block, block, block, columns, columns),
        out_specs=(block, block),
        check_vma=False,
    )
```

time: 79.9 us -> 65.8 us (0.82)
  Pallas kernels: 76.2 us -> 63.9 us
  local copies, waits for them, and re-layouts: 2.87 us -> 1.16 us
    pallas_call x1, Pallas kernels: 76.2 us -> 63.9 us  [on_device(): pl.pallas_call(functools.partial(kernel, nx, nz), out_shape=(out, out), i...]
    unnamed x4 -> x0, local copies, waits for them, and re-layouts: 2.87 us -> none
    reshape x0 -> x1, local copies, waits for them, and re-layouts: none -> 1.16 us  [on_device(): v.reshape(TILES, LAYERS, ROWS, LANES).transpose(1, 2, 0, 3)]
where the time goes in v1:
time: 65.8 us; the launch traced here: 65.7 us
  Pallas kernels  63.9 us (97%)
  local copies, waits for them, and re-layouts  1.16 us (2%)
    pallas_call x1, Pallas kernels, on_device(): pl.pallas_call(functools.partial(kernel, nx, nz), out_shape=(out, out), i...  63.9 us

profile of v1, /device:TPU:2, one launch (start us, length us, event | category | flops | bytes accessed | tf_op | source)
XLA Modules:
  0.0 65.7 jit_solution(15268804073337021708)
XLA Ops:
  0.6 63.9 %coupled_solve.1 = (f32[2,640,128]{2,1,0:T(8,128)S(1)}, f32[2,640,128]{2,1,0:T(8,128)S(1)}) custom-call(f32[640,256]{1,0:T(8,128)} %bitcast.17, bf16[640,256]{1,0:T(8,128)(2,1)} %bitcast.18, bf16[640,256]{1,0:T(8,128)(2,1)} %bitcast.19, s32[8,256]{1,0:T(8,128)} %ice_mask.1, s32[8,256]{1,0:T(8,128)} %grounded.1), custom_call_target="tpu_custom_call" | custom-call | tf_op jit(solution)/shard_map/coupled_solve/pallas_call | solution.py:431
  64.6 1.2 %copy_bitcast_fusion = (f32[1,80,8,256]{3,2,1,0:T(8,128)}, f32[1,80,8,256]{3,2,1,0:T(8,128)}) fusion(f32[2,640,128]{2,1,0:T(8,128)S(1)} %get-tuple-element.4, f32[2,640,128]{2,1,0:T(8,128)S(1)} %get-tuple-element.5), kind=kLoop, calls=%fused_computation | loop fusion | bytes 2621440 | tf_op jit(solution)/shard_map/reshape | solution.py:473

commit v2 on v1

--- a/solution.py
+++ b/solution.py
@@ -53,6 +53,9 @@
     lane3 = lax.broadcasted_iota(jnp.int32, (ROWS, SUB, LANES), 2)
     sub3 = lax.broadcasted_iota(jnp.int32, (ROWS, SUB, LANES), 1)
     lane1 = lax.broadcasted_iota(jnp.int32, (1, LANES), 1)
+
+    beside_x = (x > 0).astype(jnp.int32) + (x < nx - 1).astype(jnp.int32)
+    beside_z = (z > 0).astype(jnp.int32) + (z < nz - 1).astype(jnp.int32)
 
     def exists(d):
         dx, dz = STEPS[d]
@@ -166,10 +169,9 @@
             src, dst = pz.at[e, j], hz.at[e, j, 3 - d]
         else:
             src, dst = pc.at[e, j], hc.at[e, j, 7 - d]
-        opposite = (1, 0, 3, 2, 7, 6, 5, 4)[d]
         return pltpu.make_async_remote_copy(
             src_ref=src, dst_ref=dst, send_sem=send_sem.at[d],
-            recv_sem=recv_sem.at[e, j, opposite], device_id=at(d), device_id_type=MESH)
+            recv_sem=recv_sem.at[e % 2, j, min(d // 2, 2)], device_id=at(d), device_id_type=MESH)
 
     def store_field(f, j, parts):
         for t in range(TILES):
@@ -214,17 +216,25 @@
         pc[e, j] = jnp.sum(corners, axis=0, keepdims=True)
 
     def send_rims(e, j, wanted):
-        for d in range(8):
+        for d in (4, 5, 6, 7, 2, 3, 0, 1):
             @pl.when(exists(d) if wanted is None else jnp.logical_and(exists(d), wanted))
             def _(d=d):
                 copies(e, j, d).start()
 
     def await_rims(e, j):
-        for d in range(8):
-            @pl.when(exists(d))
-            def _(d=d):
-                opposite = (1, 0, 3, 2, 7, 6, 5, 4)[d]
-                copies(e, j, opposite).wait_recv()
+        def arrive(kind, condition, whole):
+            @pl.when(condition)
+            def _():
+                pltpu.make_async_copy(whole, whole, recv_sem.at[e % 2, j, kind]).wait()
+
+        both = beside_x * beside_z
+        arrive(0, beside_x == 2, hx.at[e, j])
+        arrive(0, beside_x == 1, hx.at[e, j, 0])
+        arrive(1, beside_z == 2, hz.at[e, j])
+        arrive(1, beside_z == 1, hz.at[e, j, 0])
+        arrive(2, both == 4, hc.at[e, j])
+        arrive(2, both == 2, hc.at[e, j, pl.ds(0, 2)])
+        arrive(2, both == 1, hc.at[e, j, 0])
 
     def spread(f, e, j):
         centre = [wbuf[f, j + 1, :, t] for t in range(TILES)]
@@ -263,8 +273,6 @@
             product = [jnp.sum(weighted[t] * wbuf[i + 1, j + 1, :, t], axis=0) for t in range(TILES)]
             acc[k, i] = acc[k, i] + (product[0] + product[1])
 
-    beside_x = (x > 0).astype(jnp.int32) + (x < nx - 1).astype(jnp.int32)
-    beside_z = (z > 0).astype(jnp.int32) + (z < nz - 1).astype(jnp.int32)
     pl.semaphore_wait(barrier, nx + nz - 1 + beside_x * beside_z)
     def first(j, carry):
         parts = [pick(cn, j, t) for t in range(TILES)]
@@ -461,7 +469,7 @@
             vmem((nz, 1, LANES), F32),
             pltpu.SemaphoreType.DMA((6,)),
             pltpu.SemaphoreType.DMA((8,)),
-            pltpu.SemaphoreType.DMA((FIELDS, CHUNKS, 8)),
+            pltpu.SemaphoreType.DMA((2, CHUNKS, 3)),
             pltpu.SemaphoreType.DMA((2,)),
             pltpu.SemaphoreType.DMA((2, 2)),
         ],

time: 65.8 us -> 61 us (0.927)
  Pallas kernels: 63.9 us -> 59.1 us
    pallas_call x1, Pallas kernels: 63.9 us -> 59.1 us  [on_device(): pl.pallas_call(functools.partial(kernel, nx, nz), out_shape=(out, out), i...]
where the time goes in v2:
time: 61 us; the launch traced here: 60.9 us
  Pallas kernels  59.1 us (97%)
  local copies, waits for them, and re-layouts  1.16 us (2%)
  between operations  0.64 us (1%)
    pallas_call x1, Pallas kernels, on_device(): pl.pallas_call(functools.partial(kernel, nx, nz), out_shape=(out, out), i...  59.1 us

profile of v2, /device:TPU:2, one launch (start us, length us, event | category | flops | bytes accessed | tf_op | source)
XLA Modules:
  0.0 60.9 jit_solution(14694630031631064844)
XLA Ops:
  0.6 59.1 %coupled_solve.1 = (f32[2,640,128]{2,1,0:T(8,128)S(1)}, f32[2,640,128]{2,1,0:T(8,128)S(1)}) custom-call(f32[640,256]{1,0:T(8,128)} %bitcast.17, bf16[640,256]{1,0:T(8,128)(2,1)} %bitcast.18, bf16[640,256]{1,0:T(8,128)(2,1)} %bitcast.19, s32[8,256]{1,0:T(8,128)} %ice_mask.1, s32[8,256]{1,0:T(8,128)} %grounded.1), custom_call_target="tpu_custom_call" | custom-call | tf_op jit(solution)/shard_map/coupled_solve/pallas_call | solution.py:439
  59.8 1.2 %copy_bitcast_fusion = (f32[1,80,8,256]{3,2,1,0:T(8,128)}, f32[1,80,8,256]{3,2,1,0:T(8,128)}) fusion(f32[2,640,128]{2,1,0:T(8,128)S(1)} %get-tuple-element.4, f32[2,640,128]{2,1,0:T(8,128)S(1)} %get-tuple-element.5), kind=kLoop, calls=%fused_computation | loop fusion | bytes 2621440 | tf_op jit(solution)/shard_map/reshape | solution.py:481

commit v3 on v2

--- a/solution.py
+++ b/solution.py
@@ -16,6 +16,7 @@
 LANES = 128
 TILES = 2
 CHUNKS = LAYERS // SUB
+EARLY = 4
 MESH = pl.DeviceIdType.MESH
 F32 = jnp.float32
 
@@ -73,6 +74,14 @@
     def at(d):
         dx, dz = STEPS[d]
         return (g, x + dx, z + dz)
+
+    barrier = pltpu.get_barrier_semaphore()
+    pl.semaphore_signal(barrier, inc=1, device_id=(g, (x + nx // 2) % nx, z), device_id_type=MESH)
+    for d in (4, 5, 6, 7, 0, 1, 2, 3):
+        @pl.when(exists(d))
+        def _(d=d):
+            pl.semaphore_signal(barrier, inc=1, device_id=at(d), device_id_type=MESH)
+    pl.semaphore_signal(barrier, inc=1, device_id=(1 - g, x, z), device_id_type=MESH)
 
     loads = [
         pltpu.make_async_copy(conduct, cbf, in_sem.at[0]),
@@ -102,28 +111,6 @@
     for d in range(8):
         zero_rims(d)
 
-    barrier = pltpu.get_barrier_semaphore()
-
-    def greet_x(i, carry):
-        @pl.when(i != x)
-        def _():
-            pl.semaphore_signal(barrier, inc=1, device_id=(g, i, z), device_id_type=MESH)
-        return carry
-
-    def greet_z(i, carry):
-        @pl.when(i != z)
-        def _():
-            pl.semaphore_signal(barrier, inc=1, device_id=(g, x, i), device_id_type=MESH)
-        return carry
-
-    lax.fori_loop(0, nx, greet_x, 0)
-    lax.fori_loop(0, nz, greet_z, 0)
-    pl.semaphore_signal(barrier, inc=1, device_id=(1 - g, x, z), device_id_type=MESH)
-    for d in range(4, 8):
-        @pl.when(exists(d))
-        def _(d=d):
-            pl.semaphore_signal(barrier, inc=1, device_id=at(d), device_id_type=MESH)
-
     acc[...] = jnp.zeros_like(acc)
 
     def clear(f, carry):
@@ -170,7 +157,7 @@
         else:
             src, dst = pc.at[e, j], hc.at[e, j, 7 - d]
         return pltpu.make_async_remote_copy(
-            src_ref=src, dst_ref=dst, send_sem=send_sem.at[d],
+            src_ref=src, dst_ref=dst, send_sem=send_sem.at[min(d // 2, 2)],
             recv_sem=recv_sem.at[e % 2, j, min(d // 2, 2)], device_id=at(d), device_id_type=MESH)
 
     def store_field(f, j, parts):
@@ -267,21 +254,33 @@
         return [beside[0] + jnp.where(lane3 < 2, rows, 0.0),
                 beside[1] + jnp.where(lane3 >= LANES - 2, rows, 0.0)]
 
-    def dots(k, j, parts, count):
-        weighted = [hbuf[j, :, t] * parts[t] for t in range(TILES)]
-        for i in range(count):
+    def dots(k, j, applied):
+        field = [wbuf[k + 1, j + 1, :, t] for t in range(TILES)]
+        weighted = [hbuf[j, :, t] * (field[t] - 0.5 * applied[t]) for t in range(TILES)]
+        for i in range(ITERS):
             product = [jnp.sum(weighted[t] * wbuf[i + 1, j + 1, :, t], axis=0) for t in range(TILES)]
             acc[k, i] = acc[k, i] + (product[0] + product[1])
-
-    pl.semaphore_wait(barrier, nx + nz - 1 + beside_x * beside_z)
+        product = [jnp.sum(hbuf[j, :, t] * field[t] * wbuf[1, j + 1, :, t], axis=0) for t in range(TILES)]
+        acc[k, ITERS] = acc[k, ITERS] + (product[0] + product[1])
+
     def first(j, carry):
         parts = [pick(cn, j, t) for t in range(TILES)]
         store_field(COUPLING, j, parts)
         pack_rims(0, j, parts)
+        return carry
+
+    def send_first(j, carry):
         send_rims(0, j, None)
         return carry
 
-    lax.fori_loop(0, CHUNKS, first, 0)
+    def first_and_send(j, carry):
+        first(j, carry)
+        return send_first(j, carry)
+
+    lax.fori_loop(0, EARLY, first, 0)
+    pl.semaphore_wait(barrier, 2 + beside_x + beside_z + beside_x * beside_z)
+    lax.fori_loop(0, EARLY, send_first, 0)
+    lax.fori_loop(EARLY, CHUNKS, first_and_send, 0)
 
     loads[3].wait()
     loads[4].wait()
@@ -330,7 +329,6 @@
             parts.append(ratio * pick(fs, j, t))
         store_field(1, j, parts)
         pack_rims(1, j, parts)
-        dots(0, j, parts, 1)
         send_rims(1, j, None)
         return carry
 
@@ -340,10 +338,11 @@
         def body(j, inner):
             await_rims(k, j)
             spreads = spread(k, k, j)
-            parts = [ebuf[j, :, t] * spreads[t] - wbuf[k - 1, j + 1, :, t] for t in range(TILES)]
+            applied = [ebuf[j, :, t] * spreads[t] for t in range(TILES)]
+            parts = [applied[t] - wbuf[k - 1, j + 1, :, t] for t in range(TILES)]
             store_field(k + 1, j, parts)
             pack_rims(k + 1, j, parts)
-            dots(k, j, parts, FIELDS)
+            dots(k - 1, j, applied)
             send_rims(k + 1, j, k < ITERS)
             return inner
 
@@ -352,9 +351,10 @@
     lax.fori_loop(1, ITERS + 1, stage, 0)
 
     gram = jnp.zeros((SUB, LANES), F32)
-    for k in range(FIELDS):
+    for k in range(ITERS):
         column = jnp.sum(jnp.sum(acc[k], axis=1), axis=1, keepdims=True)
-        gram = gram + jnp.where((lane2 == SUB * sub2 + k) & (sub2 <= k), column, 0.0)
+        wanted = (lane2 == SUB * sub2 + k) & ((sub2 <= k) | (sub2 == ITERS))
+        gram = gram + jnp.where(wanted, column, 0.0)
     row = jnp.sum(gram, axis=0, keepdims=True)
     ar_own[...] = row
 
@@ -374,14 +374,11 @@
     total = jnp.broadcast_to(total, (SUB, LANES))
 
     def entry(i, k):
-        lane = SUB * min(i, k) + max(i, k)
+        lane = SUB * i + k
         return jnp.broadcast_to(total[:, lane:lane + 1], (SUB, LANES))
 
-    gram = [[entry(i, k) for k in range(i, FIELDS)] for i in range(ITERS)]
-    inner = lambda i, k: gram[min(i, k)][abs(i - k)]
-    system = {(i, k): inner(i, k) - 0.5 * (inner(i, k + 1) + inner(i, k - 1) if k else inner(i, 1))
-              for i in range(ITERS) for k in range(i, ITERS)}
-    right = [inner(0, i) for i in range(ITERS)]
+    system = {(i, k): entry(i, k) for k in range(ITERS) for i in range(k + 1)}
+    right = [entry(ITERS, k) for k in range(ITERS)]
     inverse = []
     for p in range(ITERS):
         inverse.append(1.0 / system[p, p])
@@ -416,11 +413,19 @@
         return carry
 
     lax.fori_loop(0, CHUNKS, combine, 0)
-    for d in range(8):
-        @pl.when(exists(d))
-        def _(d=d):
-            whole = hx.at[:, :, d] if d < 2 else hz.at[:, :, d - 2] if d < 4 else hc.at[:, :, d - 4]
-            pltpu.make_async_copy(whole, whole, send_sem.at[d]).wait()
+    def left(kind, condition, whole):
+        @pl.when(condition)
+        def _():
+            pltpu.make_async_copy(whole, whole, send_sem.at[kind]).wait()
+
+    both = beside_x * beside_z
+    left(0, beside_x == 2, hx)
+    left(0, beside_x == 1, hx.at[:, :, 0])
+    left(1, beside_z == 2, hz)
+    left(1, beside_z == 1, hz.at[:, :, 0])
+    left(2, both == 4, hc)
+    left(2, both == 2, hc.at[:, :, pl.ds(0, 2)])
+    left(2, both == 1, hc.at[:, :, 0])
     sent = ar_x.at[pl.ds(0, nx - 1)]
     pltpu.make_async_copy(sent, sent, ar_sem.at[0, 0]).wait()
     sent = ar_z.at[pl.ds(0, nz - 1)]
@@ -468,7 +473,7 @@
             vmem((1, LANES), F32),
             vmem((nz, 1, LANES), F32),
             pltpu.SemaphoreType.DMA((6,)),
-            pltpu.SemaphoreType.DMA((8,)),
+            pltpu.SemaphoreType.DMA((3,)),
             pltpu.SemaphoreType.DMA((2, CHUNKS, 3)),
             pltpu.SemaphoreType.DMA((2,)),
             pltpu.SemaphoreType.DMA((2, 2)),

time: 61 us -> 60.5 us (level)
  no operation moved by 1% of the time
where the time goes in v3:
time: 60.5 us; the launch traced here: 60.4 us
  Pallas kernels  58.6 us (97%)
  local copies, waits for them, and re-layouts  1.16 us (2%)
  between operations  0.64 us (1%)
    pallas_call x1, Pallas kernels, on_device(): pl.pallas_call(functools.partial(kernel, nx, nz), out_shape=(out, out), i...  58.6 us

profile of v3, /device:TPU:2, one launch (start us, length us, event | category | flops | bytes accessed | tf_op | source)
XLA Modules:
  0.0 60.4 jit_solution(2740146185246793424)
XLA Ops:
  0.6 58.6 %coupled_solve.1 = (f32[2,640,128]{2,1,0:T(8,128)S(1)}, f32[2,640,128]{2,1,0:T(8,128)S(1)}) custom-call(f32[640,256]{1,0:T(8,128)} %bitcast.17, bf16[640,256]{1,0:T(8,128)(2,1)} %bitcast.18, bf16[640,256]{1,0:T(8,128)(2,1)} %bitcast.19, s32[8,256]{1,0:T(8,128)} %ice_mask.1, s32[8,256]{1,0:T(8,128)} %grounded.1), custom_call_target="tpu_custom_call" | custom-call | tf_op jit(solution)/shard_map/coupled_solve/pallas_call | solution.py:444
  59.2 1.2 %copy_bitcast_fusion = (f32[1,80,8,256]{3,2,1,0:T(8,128)}, f32[1,80,8,256]{3,2,1,0:T(8,128)}) fusion(f32[2,640,128]{2,1,0:T(8,128)S(1)} %get-tuple-element.4, f32[2,640,128]{2,1,0:T(8,128)S(1)} %get-tuple-element.5), kind=kLoop, calls=%fused_computation | loop fusion | bytes 2621440 | tf_op jit(solution)/shard_map/reshape | solution.py:486

commit v4 on v3

--- a/solution.py
+++ b/solution.py
@@ -16,7 +16,6 @@
 LANES = 128
 TILES = 2
 CHUNKS = LAYERS // SUB
-EARLY = 4
 MESH = pl.DeviceIdType.MESH
 F32 = jnp.float32
 
@@ -33,8 +32,13 @@
                       value.ndim - 1 if axis is None else axis)
 
 
-def far_first(count):
-    return sorted(range(1, count), key=lambda i: -min(i, count - i))
+def far_first(nx, nz):
+    def hops(step):
+        dx, dz = step
+        return min(dx % 4, -dx % 4) + min(dx // 4, 4 - dx // 4) + min(dz, nz - dz)
+
+    steps = [(dx, dz) for dx in range(nx) for dz in range(nz)]
+    return sorted(steps[1:], key=lambda step: -hops(step))
 
 
 def kernel(
@@ -42,7 +46,7 @@
     forcing, conduct, diag_add, ice_mask, grounded, out_x, out_r,
     cbf, dbf, ice_v, ground_v, active_v, fs, cn, dn,
     wbuf, hx, hz, hc, pz, pc, ebuf, hbuf, icbuf, gbuf, acc,
-    shared_out, shared_in, ar_own, ar_x, ar_own2, ar_z,
+    shared_out, shared_in, ar_own, ar_all,
     in_sem, send_sem, recv_sem, share_sem, ar_sem,
 ):
     g = lax.axis_index("group")
@@ -84,15 +88,16 @@
     pl.semaphore_signal(barrier, inc=1, device_id=(1 - g, x, z), device_id_type=MESH)
 
     loads = [
-        pltpu.make_async_copy(conduct, cbf, in_sem.at[0]),
+        pltpu.make_async_copy(conduct.at[:, pl.ds(0, ROWS)], cbf.at[:, pl.ds(0, ROWS)], in_sem.at[0]),
         pltpu.make_async_copy(ice_mask, ice_v, in_sem.at[1]),
         pltpu.make_async_copy(grounded, ground_v, in_sem.at[2]),
         pltpu.make_async_copy(forcing.at[:, pl.ds(0, LANES)], fs.at[0], in_sem.at[3]),
         pltpu.make_async_copy(forcing.at[:, pl.ds(LANES, LANES)], fs.at[1], in_sem.at[4]),
         pltpu.make_async_copy(diag_add, dbf, in_sem.at[5]),
+        pltpu.make_async_copy(conduct.at[:, pl.ds(ROWS, LAYERS - ROWS)], cbf.at[:, pl.ds(ROWS, LAYERS - ROWS)], in_sem.at[6]),
     ]
-    for load in loads:
-        load.start()
+    for n in (0, 1, 2, 6, 3, 4, 5):
+        loads[n].start()
 
     def zero_rims(d):
         @pl.when(jnp.logical_not(exists(d)))
@@ -128,19 +133,20 @@
     ground = ground_v[...].astype(F32)
     active_v[...] = ice * (1.0 - (1.0 - is_ice) * ground)
 
-    def couple(i, carry):
-        part = pl.ds(pl.multiple_of(i * SUB * ROWS, SUB * ROWS), SUB * ROWS)
-        for t in range(TILES):
-            columns = slice(t * LANES, (t + 1) * LANES)
-            value = jnp.sqrt(cbf[part, columns].astype(F32)).reshape(SUB, ROWS, LANES)
-            cn[t, part] = (value * active_v[:, columns][None]).reshape(SUB * ROWS, LANES)
-        return carry
-
-    lax.fori_loop(0, CHUNKS, couple, 0)
-
-
     def pick(ref, j, t):
         return jnp.stack([ref[t, pl.ds(j * ROWS + r, SUB, stride=CHUNKS * ROWS), :] for r in range(ROWS)])
+
+    def couple(j):
+        rows = pl.ds(pl.multiple_of(j * ROWS, ROWS), ROWS)
+        base = pl.multiple_of(j * SUB * ROWS, SUB * ROWS)
+        parts = []
+        for t in range(TILES):
+            columns = slice(t * LANES, (t + 1) * LANES)
+            value = jnp.sqrt(cbf[:, rows, columns].astype(F32)) * active_v[:, columns][None]
+            cn[t, pl.ds(base, SUB * ROWS)] = value.reshape(SUB * ROWS, LANES)
+        for t in range(TILES):
+            parts.append(jnp.stack([cn[t, pl.ds(base + r, SUB, stride=ROWS), :] for r in range(ROWS)]))
+        return parts
 
     def put(ref, j, t, value):
         for r in range(ROWS):
@@ -202,28 +208,33 @@
             corners = moved if corners is None else corners + moved
         pc[e, j] = jnp.sum(corners, axis=0, keepdims=True)
 
-    def send_rims(e, j, wanted):
+    def send_rims(e, j):
         for d in (4, 5, 6, 7, 2, 3, 0, 1):
-            @pl.when(exists(d) if wanted is None else jnp.logical_and(exists(d), wanted))
+            @pl.when(exists(d))
             def _(d=d):
                 copies(e, j, d).start()
 
+    def arrive(e, j, kind, condition, whole):
+        @pl.when(condition)
+        def _():
+            pltpu.make_async_copy(whole, whole, recv_sem.at[e % 2, j, kind]).wait()
+
     def await_rims(e, j):
-        def arrive(kind, condition, whole):
-            @pl.when(condition)
-            def _():
-                pltpu.make_async_copy(whole, whole, recv_sem.at[e % 2, j, kind]).wait()
-
+        arrive(e, j, 0, beside_x == 2, hx.at[e, j])
+        arrive(e, j, 0, beside_x == 1, hx.at[e, j, 0])
+        arrive(e, j, 1, beside_z == 2, hz.at[e, j])
+        arrive(e, j, 1, beside_z == 1, hz.at[e, j, 0])
+
+    def await_corners(e, j):
         both = beside_x * beside_z
-        arrive(0, beside_x == 2, hx.at[e, j])
-        arrive(0, beside_x == 1, hx.at[e, j, 0])
-        arrive(1, beside_z == 2, hz.at[e, j])
-        arrive(1, beside_z == 1, hz.at[e, j, 0])
-        arrive(2, both == 4, hc.at[e, j])
-        arrive(2, both == 2, hc.at[e, j, pl.ds(0, 2)])
-        arrive(2, both == 1, hc.at[e, j, 0])
-
-    def spread(f, e, j):
+        arrive(e, j, 2, both == 4, hc.at[e, j])
+        arrive(e, j, 2, both == 2, hc.at[e, j, pl.ds(0, 2)])
+        arrive(e, j, 2, both == 1, hc.at[e, j, 0])
+
+    def spread(f, e, j, late):
+        await_rims(e, j)
+        if not late:
+            await_corners(e, j)
         centre = [wbuf[f, j + 1, :, t] for t in range(TILES)]
         beside, mixed, scaled = [], [], []
         for t in range(TILES):
@@ -243,16 +254,19 @@
             beside[1] = beside[1] + jnp.where(lane3 >= LANES - shift, 0.0, b)
 
         edge = jnp.where(lane2 % 4 < 2, hz[e, j, 0], hz[e, j, 1])
-        rows = [roll(edge, -4 * (r + 1)) for r in range(ROWS)]
+        rows = jnp.stack([roll(edge, -4 * (r + 1)) for r in range(ROWS)])
+        beside[0] = beside[0] + jnp.where(lane3 < 2, rows, 0.0)
+        beside[1] = beside[1] + jnp.where(lane3 >= LANES - 2, rows, 0.0)
+        if late:
+            await_corners(e, j)
         corner = []
         for q in range(4):
             picked = jnp.where(lane2 == 8 * (3 - q) + sub2, jnp.broadcast_to(hc[e, j, q], (SUB, LANES)), 0.0)
             corner.append(jnp.sum(picked, axis=1, keepdims=True))
-        rows[0] = rows[0] + jnp.where(lane2 == 0, corner[0], jnp.where(lane2 == LANES - 1, corner[1], 0.0))
-        rows[-1] = rows[-1] + jnp.where(lane2 == 0, corner[2], jnp.where(lane2 == LANES - 1, corner[3], 0.0))
-        rows = jnp.stack(rows)
-        return [beside[0] + jnp.where(lane3 < 2, rows, 0.0),
-                beside[1] + jnp.where(lane3 >= LANES - 2, rows, 0.0)]
+        for t, lane in ((0, 0), (1, LANES - 1)):
+            low, high = [jnp.where(lane2 == lane, corner[q + t], 0.0)[None] for q in (0, 2)]
+            beside[t] = jnp.concatenate([beside[t][:1] + low, beside[t][1:-1], beside[t][-1:] + high], axis=0)
+        return beside
 
     def dots(k, j, applied):
         field = [wbuf[k + 1, j + 1, :, t] for t in range(TILES)]
@@ -263,24 +277,21 @@
         product = [jnp.sum(hbuf[j, :, t] * field[t] * wbuf[1, j + 1, :, t], axis=0) for t in range(TILES)]
         acc[k, ITERS] = acc[k, ITERS] + (product[0] + product[1])
 
-    def first(j, carry):
-        parts = [pick(cn, j, t) for t in range(TILES)]
+    def first(j):
+        parts = couple(j)
         store_field(COUPLING, j, parts)
         pack_rims(0, j, parts)
+
+    def first_and_send(j, carry):
+        first(j)
+        send_rims(0, j)
         return carry
 
-    def send_first(j, carry):
-        send_rims(0, j, None)
-        return carry
-
-    def first_and_send(j, carry):
-        first(j, carry)
-        return send_first(j, carry)
-
-    lax.fori_loop(0, EARLY, first, 0)
+    first(jnp.int32(0))
     pl.semaphore_wait(barrier, 2 + beside_x + beside_z + beside_x * beside_z)
-    lax.fori_loop(0, EARLY, send_first, 0)
-    lax.fori_loop(EARLY, CHUNKS, first_and_send, 0)
+    send_rims(0, jnp.int32(0))
+    loads[6].wait()
+    lax.fori_loop(1, CHUNKS, first_and_send, 0)
 
     loads[3].wait()
     loads[4].wait()
@@ -289,6 +300,10 @@
         mean = jnp.sum(fs[t].reshape(LAYERS, ROWS, LANES), axis=0) * (1.0 / LAYERS)
         value = active_v[:, t * LANES:(t + 1) * LANES] * mean
         shared_out[t] = value * cn[t, edge]
+    share = pltpu.make_async_remote_copy(
+        src_ref=shared_out, dst_ref=shared_in, send_sem=share_sem.at[0], recv_sem=share_sem.at[1],
+        device_id=(1 - g, x, z), device_id_type=MESH)
+    share.start()
     loads[5].wait()
 
     def widen(i, carry):
@@ -303,52 +318,72 @@
         friction = is_ice * friction_gain * (ground_v[:, columns].astype(F32) * ice_v[:, columns].astype(F32))
         dn[t, 0:ROWS] = dn[t, 0:ROWS] + friction
 
-    share = pltpu.make_async_remote_copy(
-        src_ref=shared_out, dst_ref=shared_in, send_sem=share_sem.at[0], recv_sem=share_sem.at[1],
-        device_id=(1 - g, x, z), device_id_type=MESH)
-    share.start()
-
+    def turn(source, target):
+        def body(j, carry):
+            for t in range(TILES):
+                target[j, :, t] = pick(source, j, t)
+            return carry
+
+        lax.fori_loop(0, CHUNKS, body, 0)
+
+    turn(dn, gbuf)
     share.wait()
     for t in range(TILES):
         fs[t, edge] = fs[t, edge] + shared_in[t]
-
-    def second(j, carry):
-        await_rims(0, j)
-        spreads = spread(COUPLING, 0, j)
-        parts = []
-        for t in range(TILES):
-            c = wbuf[COUPLING, j + 1, :, t]
-            diagonal = pick(dn, j, t) + c * spreads[t]
-            ratio = c / diagonal
+    turn(fs, hbuf)
+
+    def second(j, late):
+        spreads = spread(COUPLING, 0, j, late)
+        couplings = [wbuf[COUPLING, j + 1, :, t] for t in range(TILES)]
+        diagonals = [gbuf[j, :, t] + couplings[t] * spreads[t] for t in range(TILES)]
+        ratios = [couplings[t] / diagonals[t] for t in range(TILES)]
+        parts = [ratios[t] * hbuf[j, :, t] for t in range(TILES)]
+        store_field(1, j, parts)
+        pack_rims(1, j, parts)
+        for t in range(TILES):
+            c = couplings[t]
             inverse_c = jnp.where(c > 0.0, 1.0 / jnp.where(c > 0.0, c, 1.0), 0.0)
-            back = diagonal * inverse_c
-            ebuf[j, :, t] = 2.0 * ratio * c
+            back = diagonals[t] * inverse_c
+            ebuf[j, :, t] = 2.0 * ratios[t] * c
             icbuf[j, :, t] = inverse_c
             gbuf[j, :, t] = back
             hbuf[j, :, t] = back * inverse_c
-            parts.append(ratio * pick(fs, j, t))
-        store_field(1, j, parts)
-        pack_rims(1, j, parts)
-        send_rims(1, j, None)
-        return carry
-
-    lax.fori_loop(0, CHUNKS, second, 0)
-
-    def stage(k, carry):
-        def body(j, inner):
-            await_rims(k, j)
-            spreads = spread(k, k, j)
+        send_rims(1, j)
+
+    def chunks(step):
+        def body(j, carry):
+            step(j, False)
+            return carry
+
+        step(jnp.int32(0), True)
+        lax.fori_loop(1, CHUNKS, body, 0)
+
+    chunks(second)
+
+    def stage(k, last):
+        def step(j, late):
+            spreads = spread(k, k, j, late)
             applied = [ebuf[j, :, t] * spreads[t] for t in range(TILES)]
             parts = [applied[t] - wbuf[k - 1, j + 1, :, t] for t in range(TILES)]
-            store_field(k + 1, j, parts)
-            pack_rims(k + 1, j, parts)
-            dots(k - 1, j, applied)
-            send_rims(k + 1, j, k < ITERS)
-            return inner
-
-        return lax.fori_loop(0, CHUNKS, body, carry)
-
-    lax.fori_loop(1, ITERS + 1, stage, 0)
+            if last:
+                wbuf[k + 1, j + 1] = jnp.stack(parts, axis=1)
+            else:
+                store_field(k + 1, j, parts)
+                pack_rims(k + 1, j, parts)
+                if not late:
+                    dots(k - 1, j, applied)
+                send_rims(k + 1, j)
+            if last or late:
+                dots(k - 1, j, applied)
+
+        chunks(step)
+
+    def middle(k, carry):
+        stage(k, False)
+        return carry
+
+    lax.fori_loop(1, ITERS, middle, 0)
+    stage(ITERS, True)
 
     gram = jnp.zeros((SUB, LANES), F32)
     for k in range(ITERS):
@@ -357,19 +392,17 @@
         gram = gram + jnp.where(wanted, column, 0.0)
     row = jnp.sum(gram, axis=0, keepdims=True)
     ar_own[...] = row
-
-    def scatter(own, slots, me, count, offsets, device, sems):
-        for offset in offsets:
-            pltpu.make_async_remote_copy(
-                src_ref=own, dst_ref=slots.at[me], send_sem=sems.at[0], recv_sem=sems.at[1],
-                device_id=device((me + offset) % count), device_id_type=MESH).start()
-        slots[me] = own[...]
-        rest = slots.at[pl.ds(0, count - 1)]
-        pltpu.make_async_copy(rest, rest, sems.at[1]).wait()
-        return jnp.sum(slots[...], axis=0)
-
-    ar_own2[...] = scatter(ar_own, ar_x, x, nx, far_first(nx), lambda i: (g, i, z), ar_sem.at[0])
-    total = scatter(ar_own2, ar_z, z, nz, far_first(nz), lambda i: (g, x, i), ar_sem.at[1])
+    mine = x * nz + z
+    for dx, dz in far_first(nx, nz):
+        to_x, to_z = (x + dx) % nx, (z + dz) % nz
+        pltpu.make_async_remote_copy(
+            src_ref=ar_own, dst_ref=ar_all.at[mine], send_sem=ar_sem.at[0], recv_sem=ar_sem.at[1],
+            device_id=(g, to_x, to_z), device_id_type=MESH).start()
+    ar_all[mine] = row
+    rest = ar_all.at[pl.ds(0, nx * nz - 1)]
+    pltpu.make_async_copy(rest, rest, ar_sem.at[1]).wait()
+    total = ar_all[...].reshape(nx, nz, 1, LANES)
+    total = jnp.sum(jnp.sum(total, axis=0), axis=0)
 
     total = jnp.broadcast_to(total, (SUB, LANES))
 
@@ -426,10 +459,7 @@
     left(2, both == 4, hc)
     left(2, both == 2, hc.at[:, :, pl.ds(0, 2)])
     left(2, both == 1, hc.at[:, :, 0])
-    sent = ar_x.at[pl.ds(0, nx - 1)]
-    pltpu.make_async_copy(sent, sent, ar_sem.at[0, 0]).wait()
-    sent = ar_z.at[pl.ds(0, nz - 1)]
-    pltpu.make_async_copy(sent, sent, ar_sem.at[1, 0]).wait()
+    pltpu.make_async_copy(rest, rest, ar_sem.at[0]).wait()
 
 
 def on_device(nx, nz, forcing, conduct, diag_add, ice_mask, grounded):
@@ -447,7 +477,7 @@
         in_specs=[hbm_space] * 5,
         out_specs=(vmem_space, vmem_space),
         scratch_shapes=[
-            vmem((LAYERS * ROWS, wide), jnp.bfloat16),
+            vmem((SUB, CHUNKS * ROWS, wide), jnp.bfloat16),
             vmem((LAYERS * ROWS, wide), jnp.bfloat16),
             vmem((ROWS, wide), jnp.int32),
             vmem((ROWS, wide), jnp.int32),
@@ -459,8 +489,8 @@
             vmem((FIELDS, CHUNKS, 2, 2, TILES, SUB, LANES), F32),
             vmem((FIELDS, CHUNKS, 2, SUB, LANES), F32),
             vmem((FIELDS, CHUNKS, 4, 1, LANES), F32),
-            vmem((FIELDS + 1, CHUNKS, SUB, LANES), F32),
-            vmem((FIELDS + 1, CHUNKS, 1, LANES), F32),
+            vmem((FIELDS, CHUNKS, SUB, LANES), F32),
+            vmem((FIELDS, CHUNKS, 1, LANES), F32),
             vmem(field, F32),
             vmem(field, F32),
             vmem(field, F32),
@@ -469,19 +499,17 @@
             vmem((TILES, ROWS, LANES), F32),
             vmem((TILES, ROWS, LANES), F32),
             vmem((1, LANES), F32),
-            vmem((nx, 1, LANES), F32),
-            vmem((1, LANES), F32),
-            vmem((nz, 1, LANES), F32),
-            pltpu.SemaphoreType.DMA((6,)),
+            vmem((nx * nz, 1, LANES), F32),
+            pltpu.SemaphoreType.DMA((7,)),
             pltpu.SemaphoreType.DMA((3,)),
             pltpu.SemaphoreType.DMA((2, CHUNKS, 3)),
             pltpu.SemaphoreType.DMA((2,)),
-            pltpu.SemaphoreType.DMA((2, 2)),
+            pltpu.SemaphoreType.DMA((2,)),
         ],
         compiler_params=pltpu.CompilerParams(collective_id=0, has_side_effects=True, vmem_limit_bytes=40 * 1024 * 1024),
         name="coupled_solve",
     )(*[pltpu.with_memory_space_constraint(v, pltpu.HBM)
-        for v in (flat(forcing), flat(conduct), flat(diag_add), ice_mask, grounded)])
+        for v in (flat(forcing), conduct.reshape(SUB, CHUNKS * ROWS, wide), flat(diag_add), ice_mask, grounded)])
     return tuple(
         v.reshape(TILES, LAYERS, ROWS, LANES).transpose(1, 2, 0, 3).reshape(1, LAYERS, ROWS, wide)
         for v in outs)

time: 60.5 us -> 58.1 us (0.960)
  Pallas kernels: 58.6 us -> 56.2 us
    pallas_call x1, Pallas kernels: 58.6 us -> 56.2 us  [on_device(): pl.pallas_call(functools.partial(kernel, nx, nz), out_shape=(out, out), i...]
where the time goes in v4:
time: 58.1 us; the launch traced here: 58 us
  Pallas kernels  56.2 us (97%)
  local copies, waits for them, and re-layouts  1.16 us (2%)
  between operations  0.64 us (1%)
    pallas_call x1, Pallas kernels, on_device(): pl.pallas_call(functools.partial(kernel, nx, nz), out_shape=(out, out), i...  56.2 us

profile of v4, /device:TPU:2, one launch (start us, length us, event | category | flops | bytes accessed | tf_op | source)
XLA Modules:
  0.0 58.0 jit_solution(7884615225193697059)
XLA Ops:
  0.6 56.2 %coupled_solve.1 = (f32[2,640,128]{2,1,0:T(8,128)S(1)}, f32[2,640,128]{2,1,0:T(8,128)S(1)}) custom-call(f32[640,256]{1,0:T(8,128)} %bitcast.17, bf16[8,80,256]{2,1,0:T(8,128)(2,1)} %bitcast.18, bf16[640,256]{1,0:T(8,128)(2,1)} %bitcast.19, s32[8,256]{1,0:T(8,128)} %ice_mask.1, s32[8,256]{1,0:T(8,128)} %grounded.1), custom_call_target="tpu_custom_call" | custom-call | tf_op jit(solution)/shard_map/coupled_solve/pallas_call | solution.py:474
  56.8 1.2 %copy_bitcast_fusion = (f32[1,80,8,256]{3,2,1,0:T(8,128)}, f32[1,80,8,256]{3,2,1,0:T(8,128)}) fusion(f32[2,640,128]{2,1,0:T(8,128)S(1)} %get-tuple-element.4, f32[2,640,128]{2,1,0:T(8,128)S(1)} %get-tuple-element.5), kind=kLoop, calls=%fused_computation | loop fusion | bytes 2621440 | tf_op jit(solution)/shard_map/reshape | solution.py:514

commit v5 on v4

--- a/solution.py
+++ b/solution.py
@@ -9,6 +9,7 @@
 
 ITERS = 6
 FIELDS = ITERS + 1
+CORNERED = FIELDS - 1
 COUPLING = FIELDS + 1
 LAYERS = 80
 ROWS = 8
@@ -45,9 +46,9 @@
     nx, nz,
     forcing, conduct, diag_add, ice_mask, grounded, out_x, out_r,
     cbf, dbf, ice_v, ground_v, active_v, fs, cn, dn,
-    wbuf, hx, hz, hc, pz, pc, ebuf, hbuf, icbuf, gbuf, acc,
+    wbuf, hx, hz, hc, pz, pc, ebuf, hbuf, icbuf, gbuf, wcbuf, ecbuf, acc,
     shared_out, shared_in, ar_own, ar_all,
-    in_sem, send_sem, recv_sem, share_sem, ar_sem,
+    in_sem, send_sem, recv_sem, corner_sem, share_sem, ar_sem,
 ):
     g = lax.axis_index("group")
     x = lax.axis_index("gx")
@@ -80,7 +81,10 @@
         return (g, x + dx, z + dz)
 
     barrier = pltpu.get_barrier_semaphore()
-    pl.semaphore_signal(barrier, inc=1, device_id=(g, (x + nx // 2) % nx, z), device_id_type=MESH)
+    far = sorted({(a * nx // 4, b * nz // 2) for a in range(4) for b in range(2)} - {(0, 0)})
+    for dx, dz in far:
+        pl.semaphore_signal(
+            barrier, inc=1, device_id=(g, (x + dx) % nx, (z + dz) % nz), device_id_type=MESH)
     for d in (4, 5, 6, 7, 0, 1, 2, 3):
         @pl.when(exists(d))
         def _(d=d):
@@ -111,7 +115,7 @@
                 else:
                     hc[e, :, d - 4] = jnp.zeros((CHUNKS, 1, LANES), F32)
                 return carry
-            lax.fori_loop(0, FIELDS, body, 0)
+            lax.fori_loop(0, FIELDS if d < 4 else CORNERED, body, 0)
 
     for d in range(8):
         zero_rims(d)
@@ -124,6 +128,7 @@
         return carry
 
     lax.fori_loop(0, FIELDS + 1, clear, 0)
+    wcbuf[0] = jnp.zeros((CHUNKS + 2, 2, SUB, LANES), F32)
 
     loads[0].wait()
     loads[1].wait()
@@ -164,7 +169,8 @@
             src, dst = pc.at[e, j], hc.at[e, j, 7 - d]
         return pltpu.make_async_remote_copy(
             src_ref=src, dst_ref=dst, send_sem=send_sem.at[min(d // 2, 2)],
-            recv_sem=recv_sem.at[e % 2, j, min(d // 2, 2)], device_id=at(d), device_id_type=MESH)
+            recv_sem=recv_sem.at[e % 2, j, d // 2] if d < 4 else corner_sem.at[e % 4, j],
+            device_id=at(d), device_id_type=MESH)
 
     def store_field(f, j, parts):
         for t in range(TILES):
@@ -180,7 +186,21 @@
             for t in range(TILES):
                 wbuf[f, 0, :, t] = jnp.where(sub3 > 0, roll(parts[t], 1, 1), 0.0)
 
-    def pack_rims(e, j, parts):
+    def store_corners(f, j, corners):
+        for p in range(2):
+            wcbuf[f, j + 1, p] = corners[p]
+
+        @pl.when(j == 0)
+        def _():
+            for p in range(2):
+                wcbuf[f, CHUNKS + 1, p] = jnp.where(sub2 < SUB - 1, roll(corners[p], SUB - 1, 0), 0.0)
+
+        @pl.when(j == CHUNKS - 1)
+        def _():
+            for p in range(2):
+                wcbuf[f, 0, p] = jnp.where(sub2 > 0, roll(corners[p], 1, 0), 0.0)
+
+    def pack_rims(e, j, parts, raw=None, ahead=True, scale=None):
         none = jnp.zeros((1, SUB, LANES), F32)
         crossed, scaled = [], []
         for t in range(TILES):
@@ -198,43 +218,93 @@
             for r in range(ROWS):
                 moved = roll(source[r], 4 * (r + 1) + shift)
                 packed = moved if packed is None else packed + moved
+        for base, row, inner in ((0, 0, 1), (4 * (ROWS + 1), ROWS - 1, ROWS - 2)):
+            for tile, lane, way in ((1, LANES - 1, 1), (0, 0, -1)):
+                straight = parts[tile][row] + far_weight * parts[tile][inner]
+                packed = packed + roll(jnp.where(lane2 == lane, straight, 0.0), base + way)
+                across = jnp.where(lane2 == lane - way, cross_weight * parts[tile][row], 0.0)
+                packed = packed + roll(across, base + 2 * way)
         pz[e, j] = packed
-        corners = None
+        moved = []
+
+        def place(value, lane, target):
+            only = jnp.where(lane2 == lane, value, 0.0)
+            moved.append(pltpu.roll(only, (target - lane) % LANES, 1, stride=1, stride_axis=0))
+
         for q in range(4):
-            row, tile = (0, ROWS - 1)[q // 2], q % 2
-            lane = (0, LANES - 1)[tile]
-            only = jnp.where(lane2 == lane, cross_weight * parts[tile][row], 0.0)
-            moved = pltpu.roll(only, (8 * q - lane) % LANES, 1, stride=1, stride_axis=0)
-            corners = moved if corners is None else corners + moved
-        pc[e, j] = jnp.sum(corners, axis=0, keepdims=True)
-
-    def send_rims(e, j):
-        for d in (4, 5, 6, 7, 2, 3, 0, 1):
-            @pl.when(exists(d))
+            tile = q % 2
+            lane, way = ((0, 1), (LANES - 1, -1))[tile]
+            edge, one, two = ((0, 1, 2), (ROWS - 1, ROWS - 2, ROWS - 3))[q // 2]
+            field = parts[tile]
+            if raw is not None:
+                place(field[edge], lane, 8 * q)
+            if ahead:
+                place(field[one] + far_weight * field[two], lane, 32 + 8 * q)
+                place(field[edge] + cross_weight * field[one], lane + way, 32 + 8 * q)
+                place(far_weight * field[edge], lane + 2 * way, 32 + 8 * q)
+            if scale is not None:
+                place(scale[tile][edge], lane, 64 + 8 * q)
+        pc[e, j] = jnp.sum(functools.reduce(jnp.add, moved), axis=0, keepdims=True)
+
+    def send_rims(e, j, directions, wanted=None):
+        for d in directions:
+            @pl.when(exists(d) if wanted is None else jnp.logical_and(exists(d), wanted))
             def _(d=d):
                 copies(e, j, d).start()
 
-    def arrive(e, j, kind, condition, whole):
+    ALONG_X, BESIDE = (0, 1), (2, 3, 4, 5, 6, 7)
+
+    def arrive(semaphore, condition, whole):
         @pl.when(condition)
         def _():
-            pltpu.make_async_copy(whole, whole, recv_sem.at[e % 2, j, kind]).wait()
+            pltpu.make_async_copy(whole, whole, semaphore).wait()
 
     def await_rims(e, j):
-        arrive(e, j, 0, beside_x == 2, hx.at[e, j])
-        arrive(e, j, 0, beside_x == 1, hx.at[e, j, 0])
-        arrive(e, j, 1, beside_z == 2, hz.at[e, j])
-        arrive(e, j, 1, beside_z == 1, hz.at[e, j, 0])
-
-    def await_corners(e, j):
-        both = beside_x * beside_z
-        arrive(e, j, 2, both == 4, hc.at[e, j])
-        arrive(e, j, 2, both == 2, hc.at[e, j, pl.ds(0, 2)])
-        arrive(e, j, 2, both == 1, hc.at[e, j, 0])
-
-    def spread(f, e, j, late):
-        await_rims(e, j)
-        if not late:
-            await_corners(e, j)
+        arrive(recv_sem.at[e % 2, j, 0], beside_x == 2, hx.at[e, j])
+        arrive(recv_sem.at[e % 2, j, 0], beside_x == 1, hx.at[e, j, 0])
+        arrive(recv_sem.at[e % 2, j, 1], beside_z == 2, hz.at[e, j])
+        arrive(recv_sem.at[e % 2, j, 1], beside_z == 1, hz.at[e, j, 0])
+
+    def await_corners(e, j, wanted=None):
+        def when(count):
+            here = beside_x * beside_z == count
+            return here if wanted is None else jnp.logical_and(here, wanted)
+
+        arrive(corner_sem.at[e % 4, j], when(4), hc.at[e, j])
+        arrive(corner_sem.at[e % 4, j], when(2), hc.at[e, j, pl.ds(0, 2)])
+        arrive(corner_sem.at[e % 4, j], when(1), hc.at[e, j, 0])
+
+    def corner_values(e, j, base):
+        values = []
+        for q in range(4):
+            here = lane2 == base + 8 * (3 - q) + sub2
+            picked = jnp.where(here, jnp.broadcast_to(hc[e, j, q], (SUB, LANES)), 0.0)
+            values.append(jnp.sum(picked, axis=1, keepdims=True))
+        return [at_ends(jnp.broadcast_to(values[2 * p], (SUB, LANES)),
+                        jnp.broadcast_to(values[2 * p + 1], (SUB, LANES))) for p in range(2)]
+
+    def at_ends(low, high):
+        return jnp.where(lane2 == 0, low, jnp.where(lane2 == LANES - 1, high, 0.0))
+
+    def next_corners(k, j):
+        e = k - 1
+        alone = corner_values(e, j, 32)
+        edge = jnp.where(lane2 % 4 < 2, hz[e, j, 0], hz[e, j, 1])
+        corners = []
+        for p in range(2):
+            near = [hx[e, j, p, 1 - p, t] for t in range(TILES)]
+            outer = [hx[e, j, p, p, t] for t in range(TILES)]
+            row = p * (ROWS - 1)
+            total = at_ends(near[0], near[1]) + cross_weight * at_ends(outer[0], outer[1])
+            total = total + far_weight * at_ends(roll(near[0], -1), roll(near[1], 1))
+            total = total + cross_weight * at_ends(wbuf[e, j + 1, row, 0], wbuf[e, j + 1, row, 1])
+            beyond = edge if p == 0 else roll(edge, -4 * (ROWS + 1))
+            total = total + at_ends(beyond, beyond) + alone[p]
+            total = total + vertical_weight * (wcbuf[k - 1, j, p] + wcbuf[k - 1, j + 2, p])
+            corners.append(ecbuf[j, p] * total - wcbuf[k - 2, j + 1, p])
+        return corners
+
+    def spread(f, e, j, corners):
         centre = [wbuf[f, j + 1, :, t] for t in range(TILES)]
         beside, mixed, scaled = [], [], []
         for t in range(TILES):
@@ -254,19 +324,13 @@
             beside[1] = beside[1] + jnp.where(lane3 >= LANES - shift, 0.0, b)
 
         edge = jnp.where(lane2 % 4 < 2, hz[e, j, 0], hz[e, j, 1])
-        rows = jnp.stack([roll(edge, -4 * (r + 1)) for r in range(ROWS)])
-        beside[0] = beside[0] + jnp.where(lane3 < 2, rows, 0.0)
-        beside[1] = beside[1] + jnp.where(lane3 >= LANES - 2, rows, 0.0)
-        if late:
-            await_corners(e, j)
-        corner = []
-        for q in range(4):
-            picked = jnp.where(lane2 == 8 * (3 - q) + sub2, jnp.broadcast_to(hc[e, j, q], (SUB, LANES)), 0.0)
-            corner.append(jnp.sum(picked, axis=1, keepdims=True))
-        for t, lane in ((0, 0), (1, LANES - 1)):
-            low, high = [jnp.where(lane2 == lane, corner[q + t], 0.0)[None] for q in (0, 2)]
-            beside[t] = jnp.concatenate([beside[t][:1] + low, beside[t][1:-1], beside[t][-1:] + high], axis=0)
-        return beside
+        rows = [roll(edge, -4 * (r + 1)) for r in range(ROWS)]
+        corners = corners() if callable(corners) else corners
+        rows[0] = rows[0] + cross_weight * corners[0]
+        rows[-1] = rows[-1] + cross_weight * corners[1]
+        rows = jnp.stack(rows)
+        return [beside[0] + jnp.where(lane3 < 2, rows, 0.0),
+                beside[1] + jnp.where(lane3 >= LANES - 2, rows, 0.0)]
 
     def dots(k, j, applied):
         field = [wbuf[k + 1, j + 1, :, t] for t in range(TILES)]
@@ -280,16 +344,16 @@
     def first(j):
         parts = couple(j)
         store_field(COUPLING, j, parts)
-        pack_rims(0, j, parts)
+        pack_rims(0, j, parts, raw=True, ahead=False)
 
     def first_and_send(j, carry):
         first(j)
-        send_rims(0, j)
+        send_rims(0, j, BESIDE + ALONG_X)
         return carry
 
     first(jnp.int32(0))
-    pl.semaphore_wait(barrier, 2 + beside_x + beside_z + beside_x * beside_z)
-    send_rims(0, jnp.int32(0))
+    pl.semaphore_wait(barrier, 1 + len(far) + beside_x + beside_z + beside_x * beside_z)
+    send_rims(0, jnp.int32(0), BESIDE[2:] + BESIDE[:2] + ALONG_X)
     loads[6].wait()
     lax.fori_loop(1, CHUNKS, first_and_send, 0)
 
@@ -333,22 +397,25 @@
     turn(fs, hbuf)
 
     def second(j, late):
-        spreads = spread(COUPLING, 0, j, late)
+        await_rims(0, j)
+        await_corners(0, j)
+        spreads = spread(COUPLING, 0, j, corner_values(0, j, 0))
         couplings = [wbuf[COUPLING, j + 1, :, t] for t in range(TILES)]
         diagonals = [gbuf[j, :, t] + couplings[t] * spreads[t] for t in range(TILES)]
         ratios = [couplings[t] / diagonals[t] for t in range(TILES)]
         parts = [ratios[t] * hbuf[j, :, t] for t in range(TILES)]
         store_field(1, j, parts)
-        pack_rims(1, j, parts)
+        scale = [2.0 * ratios[t] * couplings[t] for t in range(TILES)]
+        pack_rims(1, j, parts, raw=True, scale=scale)
         for t in range(TILES):
             c = couplings[t]
             inverse_c = jnp.where(c > 0.0, 1.0 / jnp.where(c > 0.0, c, 1.0), 0.0)
             back = diagonals[t] * inverse_c
-            ebuf[j, :, t] = 2.0 * ratios[t] * c
+            ebuf[j, :, t] = scale[t]
             icbuf[j, :, t] = inverse_c
             gbuf[j, :, t] = back
             hbuf[j, :, t] = back * inverse_c
-        send_rims(1, j)
+        send_rims(1, j, BESIDE[2:] + BESIDE[:2] + ALONG_X)
 
     def chunks(step):
         def body(j, carry):
@@ -360,30 +427,54 @@
 
     chunks(second)
 
-    def stage(k, last):
+    def stage(k, place):
         def step(j, late):
-            spreads = spread(k, k, j, late)
+            if place == "first":
+                await_rims(k, j)
+                await_corners(k, j)
+                corners = corner_values(k, j, 0)
+                scales = corner_values(k, j, 64)
+                for p in range(2):
+                    ecbuf[j, p] = scales[p]
+            else:
+                if not late:
+                    await_rims(k, j)
+                await_corners(k - 1, j, None if place == "last" else k > 2)
+                corners = next_corners(k, j)
+                if late:
+                    store_corners(k, j, corners)
+                    await_rims(k, j)
+            spreads = spread(k, k, j, corners)
             applied = [ebuf[j, :, t] * spreads[t] for t in range(TILES)]
             parts = [applied[t] - wbuf[k - 1, j + 1, :, t] for t in range(TILES)]
-            if last:
-                wbuf[k + 1, j + 1] = jnp.stack(parts, axis=1)
-            else:
-                store_field(k + 1, j, parts)
-                pack_rims(k + 1, j, parts)
-                if not late:
-                    dots(k - 1, j, applied)
-                send_rims(k + 1, j)
-            if last or late:
+            if place == "last":
+                for t in range(TILES):
+                    wbuf[k + 1, j + 1, :, t] = parts[t]
                 dots(k - 1, j, applied)
+                return
+            store_field(k + 1, j, parts)
+            if late:
+                send_rims(k + 1, j, ALONG_X)
+            pack_rims(k + 1, j, parts)
+            if place == "first" or not late:
+                store_corners(k, j, corners)
+            if not late:
+                dots(k - 1, j, applied)
+                send_rims(k + 1, j, ALONG_X)
+            send_rims(k + 1, j, BESIDE[:2])
+            send_rims(k + 1, j, BESIDE[2:], None if place == "first" else k < ITERS - 1)
+            if late:
+                dots(k - 1, j, applied)
 
         chunks(step)
 
     def middle(k, carry):
-        stage(k, False)
+        stage(k, "middle")
         return carry
 
-    lax.fori_loop(1, ITERS, middle, 0)
-    stage(ITERS, True)
+    stage(1, "first")
+    lax.fori_loop(2, ITERS, middle, 0)
+    stage(ITERS, "last")
 
     gram = jnp.zeros((SUB, LANES), F32)
     for k in range(ITERS):
@@ -488,13 +579,15 @@
             vmem((COUPLING + 1, CHUNKS + 2, ROWS, TILES, SUB, LANES), F32),
             vmem((FIELDS, CHUNKS, 2, 2, TILES, SUB, LANES), F32),
             vmem((FIELDS, CHUNKS, 2, SUB, LANES), F32),
-            vmem((FIELDS, CHUNKS, 4, 1, LANES), F32),
+            vmem((CORNERED, CHUNKS, 4, 1, LANES), F32),
             vmem((FIELDS, CHUNKS, SUB, LANES), F32),
             vmem((FIELDS, CHUNKS, 1, LANES), F32),
             vmem(field, F32),
             vmem(field, F32),
             vmem(field, F32),
             vmem(field, F32),
+            vmem((FIELDS, CHUNKS + 2, 2, SUB, LANES), F32),
+            vmem((CHUNKS, 2, SUB, LANES), F32),
             vmem((SUB, SUB, SUB, LANES), F32),
             vmem((TILES, ROWS, LANES), F32),
             vmem((TILES, ROWS, LANES), F32),
@@ -502,7 +595,8 @@
             vmem((nx * nz, 1, LANES), F32),
             pltpu.SemaphoreType.DMA((7,)),
             pltpu.SemaphoreType.DMA((3,)),
-            pltpu.SemaphoreType.DMA((2, CHUNKS, 3)),
+            pltpu.SemaphoreType.DMA((2, CHUNKS, 2)),
+            pltpu.SemaphoreType.DMA((4, CHUNKS)),
             pltpu.SemaphoreType.DMA((2,)),
             pltpu.SemaphoreType.DMA((2,)),
         ],

time: 58.1 us -> 55 us (0.947)
  Pallas kernels: 56.2 us -> 53.1 us
    pallas_call x1, Pallas kernels: 56.2 us -> 53.1 us  [on_device(): pl.pallas_call(functools.partial(kernel, nx, nz), out_shape=(out, out), i...]
where the time goes in v5:
time: 55 us; the launch traced here: 54.9 us
  Pallas kernels  53.1 us (97%)
  local copies, waits for them, and re-layouts  1.16 us (2%)
  between operations  0.64 us (1%)
    pallas_call x1, Pallas kernels, on_device(): pl.pallas_call(functools.partial(kernel, nx, nz), out_shape=(out, out), i...  53.1 us
    reshape x1, local copies, waits for them, and re-layouts, on_device(): v.reshape(TILES, LAYERS, ROWS, LANES).transpose(1, 2, 0, 3)  1.16 us

profile of v5, /device:TPU:2, one launch (start us, length us, event | category | flops | bytes accessed | tf_op | source)
XLA Modules:
  0.0 54.9 jit_solution(11427479899419169981)
XLA Ops:
  0.6 53.1 %coupled_solve.1 = (f32[2,640,128]{2,1,0:T(8,128)S(1)}, f32[2,640,128]{2,1,0:T(8,128)S(1)}) custom-call(f32[640,256]{1,0:T(8,128)} %bitcast.17, bf16[8,80,256]{2,1,0:T(8,128)(2,1)} %bitcast.18, bf16[640,256]{1,0:T(8,128)(2,1)} %bitcast.19, s32[8,256]{1,0:T(8,128)} %ice_mask.1, s32[8,256]{1,0:T(8,128)} %grounded.1), custom_call_target="tpu_custom_call" | custom-call | tf_op jit(solution)/shard_map/coupled_solve/pallas_call | solution.py:565
  53.8 1.2 %copy_bitcast_fusion = (f32[1,80,8,256]{3,2,1,0:T(8,128)}, f32[1,80,8,256]{3,2,1,0:T(8,128)}) fusion(f32[2,640,128]{2,1,0:T(8,128)S(1)} %get-tuple-element.4, f32[2,640,128]{2,1,0:T(8,128)S(1)} %get-tuple-element.5), kind=kLoop, calls=%fused_computation | loop fusion | bytes 2621440 | tf_op jit(solution)/shard_map/reshape | solution.py:608

commit v6 on v5

--- a/solution.py
+++ b/solution.py
@@ -17,6 +17,7 @@
 LANES = 128
 TILES = 2
 CHUNKS = LAYERS // SUB
+HALF = CHUNKS // 2
 MESH = pl.DeviceIdType.MESH
 F32 = jnp.float32
 
@@ -46,9 +47,9 @@
     nx, nz,
     forcing, conduct, diag_add, ice_mask, grounded, out_x, out_r,
     cbf, dbf, ice_v, ground_v, active_v, fs, cn, dn,
-    wbuf, hx, hz, hc, pz, pc, ebuf, hbuf, icbuf, gbuf, wcbuf, ecbuf, acc,
+    wbuf, hx, hz, hc, pz, pc, ebuf, hbuf, icbuf, gbuf, wcbuf, ecbuf, abuf, acc,
     shared_out, shared_in, ar_own, ar_all,
-    in_sem, send_sem, recv_sem, corner_sem, share_sem, ar_sem,
+    in_sem, send_sem, recv_sem, corner_sem, half_sem, share_sem, ar_sem, far_sem,
 ):
     g = lax.axis_index("group")
     x = lax.axis_index("gx")
@@ -81,10 +82,7 @@
         return (g, x + dx, z + dz)
 
     barrier = pltpu.get_barrier_semaphore()
-    far = sorted({(a * nx // 4, b * nz // 2) for a in range(4) for b in range(2)} - {(0, 0)})
-    for dx, dz in far:
-        pl.semaphore_signal(
-            barrier, inc=1, device_id=(g, (x + dx) % nx, (z + dz) % nz), device_id_type=MESH)
+    pl.semaphore_signal(barrier, inc=1, device_id=(g, (x + nx // 2) % nx, z), device_id_type=MESH)
     for d in (4, 5, 6, 7, 0, 1, 2, 3):
         @pl.when(exists(d))
         def _(d=d):
@@ -169,7 +167,7 @@
             src, dst = pc.at[e, j], hc.at[e, j, 7 - d]
         return pltpu.make_async_remote_copy(
             src_ref=src, dst_ref=dst, send_sem=send_sem.at[min(d // 2, 2)],
-            recv_sem=recv_sem.at[e % 2, j, d // 2] if d < 4 else corner_sem.at[e % 4, j],
+            recv_sem=recv_sem.at[e % 2, j, d // 2] if d < 4 else corner_sem.at[e % 2, j],
             device_id=at(d), device_id_type=MESH)
 
     def store_field(f, j, parts):
@@ -265,14 +263,28 @@
         arrive(recv_sem.at[e % 2, j, 1], beside_z == 2, hz.at[e, j])
         arrive(recv_sem.at[e % 2, j, 1], beside_z == 1, hz.at[e, j, 0])
 
-    def await_corners(e, j, wanted=None):
-        def when(count):
-            here = beside_x * beside_z == count
-            return here if wanted is None else jnp.logical_and(here, wanted)
-
-        arrive(corner_sem.at[e % 4, j], when(4), hc.at[e, j])
-        arrive(corner_sem.at[e % 4, j], when(2), hc.at[e, j, pl.ds(0, 2)])
-        arrive(corner_sem.at[e % 4, j], when(1), hc.at[e, j, 0])
+    def await_corners(e, j):
+        both = beside_x * beside_z
+        arrive(corner_sem.at[e % 2, j], both == 4, hc.at[e, j])
+        arrive(corner_sem.at[e % 2, j], both == 2, hc.at[e, j, pl.ds(0, 2)])
+        arrive(corner_sem.at[e % 2, j], both == 1, hc.at[e, j, 0])
+
+    def await_half(e, half, wanted):
+        both, part = beside_x * beside_z, pl.ds(half * HALF, HALF)
+        semaphore = half_sem.at[e % 4, half]
+        arrive(semaphore, jnp.logical_and(both == 4, wanted), hc.at[e, part])
+        arrive(semaphore, jnp.logical_and(both == 2, wanted), hc.at[e, part, pl.ds(0, 2)])
+        arrive(semaphore, jnp.logical_and(both == 1, wanted), hc.at[e, part, 0])
+
+    def send_half(e, half, wanted):
+        part = pl.ds(half * HALF, HALF)
+        for d in range(4, 8):
+            @pl.when(jnp.logical_and(exists(d), wanted))
+            def _(d=d):
+                pltpu.make_async_remote_copy(
+                    src_ref=pc.at[e, part], dst_ref=hc.at[e, part, 7 - d],
+                    send_sem=send_sem.at[2], recv_sem=half_sem.at[e % 4, half],
+                    device_id=at(d), device_id_type=MESH).start()
 
     def corner_values(e, j, base):
         values = []
@@ -352,7 +364,7 @@
         return carry
 
     first(jnp.int32(0))
-    pl.semaphore_wait(barrier, 1 + len(far) + beside_x + beside_z + beside_x * beside_z)
+    pl.semaphore_wait(barrier, 2 + beside_x + beside_z + beside_x * beside_z)
     send_rims(0, jnp.int32(0), BESIDE[2:] + BESIDE[:2] + ALONG_X)
     loads[6].wait()
     lax.fori_loop(1, CHUNKS, first_and_send, 0)
@@ -429,21 +441,24 @@
 
     def stage(k, place):
         def step(j, late):
+            if not late:
+                await_rims(k, j)
             if place == "first":
-                await_rims(k, j)
                 await_corners(k, j)
                 corners = corner_values(k, j, 0)
                 scales = corner_values(k, j, 64)
                 for p in range(2):
                     ecbuf[j, p] = scales[p]
             else:
-                if not late:
-                    await_rims(k, j)
-                await_corners(k - 1, j, None if place == "last" else k > 2)
+                ahead = jnp.bool_(True) if place == "last" else k > 2
+                if late:
+                    await_half(k - 1, 0, ahead)
+                else:
+                    await_half(k - 1, 1, jnp.logical_and(ahead, j == HALF))
                 corners = next_corners(k, j)
-                if late:
-                    store_corners(k, j, corners)
-                    await_rims(k, j)
+            if late:
+                store_corners(k, j, corners)
+                await_rims(k, j)
             spreads = spread(k, k, j, corners)
             applied = [ebuf[j, :, t] * spreads[t] for t in range(TILES)]
             parts = [applied[t] - wbuf[k - 1, j + 1, :, t] for t in range(TILES)]
@@ -452,21 +467,28 @@
                     wbuf[k + 1, j + 1, :, t] = parts[t]
                 dots(k - 1, j, applied)
                 return
+            if not late:
+                rest(j - 1)
+            for t in range(TILES):
+                abuf[:, t] = applied[t]
             store_field(k + 1, j, parts)
-            if late:
-                send_rims(k + 1, j, ALONG_X)
-            pack_rims(k + 1, j, parts)
-            if place == "first" or not late:
+            send_rims(k + 1, j, ALONG_X)
+            if not late:
                 store_corners(k, j, corners)
-            if not late:
-                dots(k - 1, j, applied)
-                send_rims(k + 1, j, ALONG_X)
-            send_rims(k + 1, j, BESIDE[:2])
-            send_rims(k + 1, j, BESIDE[2:], None if place == "first" else k < ITERS - 1)
-            if late:
-                dots(k - 1, j, applied)
-
+                send_rims(k + 1, j - 1, BESIDE[:2])
+                send_half(k + 1, 0, jnp.logical_and(j == HALF, sends_corners))
+
+        def rest(j):
+            pack_rims(k + 1, j, [wbuf[k + 1, j + 1, :, t] for t in range(TILES)])
+            dots(k - 1, j, [abuf[:, t] for t in range(TILES)])
+
+        sends_corners = jnp.bool_(True) if place == "first" else k < ITERS - 1
         chunks(step)
+        if place != "last":
+            final = jnp.int32(CHUNKS - 1)
+            rest(final)
+            send_rims(k + 1, final, BESIDE[:2])
+            send_half(k + 1, 1, sends_corners)
 
     def middle(k, carry):
         stage(k, "middle")
@@ -474,7 +496,13 @@
 
     stage(1, "first")
     lax.fori_loop(2, ITERS, middle, 0)
+    far = {(0, nz // 2)} | {(a * nx // 4, 0) for a in range(4)} | {(nx // 2, nz // 2)}
+    far = sorted(far - {(0, 0)})
+    for dx, dz in far:
+        pl.semaphore_signal(
+            far_sem, inc=1, device_id=(g, (x + dx) % nx, (z + dz) % nz), device_id_type=MESH)
     stage(ITERS, "last")
+    pl.semaphore_wait(far_sem, len(far))
 
     gram = jnp.zeros((SUB, LANES), F32)
     for k in range(ITERS):
@@ -588,6 +616,7 @@
             vmem(field, F32),
             vmem((FIELDS, CHUNKS + 2, 2, SUB, LANES), F32),
             vmem((CHUNKS, 2, SUB, LANES), F32),
+            vmem((ROWS, TILES, SUB, LANES), F32),
             vmem((SUB, SUB, SUB, LANES), F32),
             vmem((TILES, ROWS, LANES), F32),
             vmem((TILES, ROWS, LANES), F32),
@@ -596,9 +625,11 @@
             pltpu.SemaphoreType.DMA((7,)),
             pltpu.SemaphoreType.DMA((3,)),
             pltpu.SemaphoreType.DMA((2, CHUNKS, 2)),
-            pltpu.SemaphoreType.DMA((4, CHUNKS)),
+            pltpu.SemaphoreType.DMA((2, CHUNKS)),
+            pltpu.SemaphoreType.DMA((4, 2)),
             pltpu.SemaphoreType.DMA((2,)),
             pltpu.SemaphoreType.DMA((2,)),
+            pltpu.SemaphoreType.REGULAR,
         ],
         compiler_params=pltpu.CompilerParams(collective_id=0, has_side_effects=True, vmem_limit_bytes=40 * 1024 * 1024),
         name="coupled_solve",

time: 55 us -> 53.5 us (0.973)
  Pallas kernels: 53.1 us -> 51.6 us
    pallas_call x1, Pallas kernels: 53.1 us -> 51.6 us  [on_device(): pl.pallas_call(functools.partial(kernel, nx, nz), out_shape=(out, out), i...]
where the time goes in v6:
time: 53.5 us; the launch traced here: 53.4 us
  Pallas kernels  51.6 us (96%)
  local copies, waits for them, and re-layouts  1.16 us (2%)
  between operations  0.64 us (1%)
    pallas_call x1, Pallas kernels, on_device(): pl.pallas_call(functools.partial(kernel, nx, nz), out_shape=(out, out), i...  51.6 us
    reshape x1, local copies, waits for them, and re-layouts, on_device(): v.reshape(TILES, LAYERS, ROWS, LANES).transpose(1, 2, 0, 3)  1.16 us

profile of v6, /device:TPU:2, one launch (start us, length us, event | category | flops | bytes accessed | tf_op | source)
XLA Modules:
  0.0 53.4 jit_solution(17055974174794842690)
XLA Ops:
  0.6 51.6 %coupled_solve.1 = (f32[2,640,128]{2,1,0:T(8,128)S(1)}, f32[2,640,128]{2,1,0:T(8,128)S(1)}) custom-call(f32[640,256]{1,0:T(8,128)} %bitcast.17, bf16[8,80,256]{2,1,0:T(8,128)(2,1)} %bitcast.18, bf16[640,256]{1,0:T(8,128)(2,1)} %bitcast.19, s32[8,256]{1,0:T(8,128)} %ice_mask.1, s32[8,256]{1,0:T(8,128)} %grounded.1), custom_call_target="tpu_custom_call" | custom-call | tf_op jit(solution)/shard_map/coupled_solve/pallas_call | solution.py:593
  52.2 1.2 %copy_bitcast_fusion = (f32[1,80,8,256]{3,2,1,0:T(8,128)}, f32[1,80,8,256]{3,2,1,0:T(8,128)}) fusion(f32[2,640,128]{2,1,0:T(8,128)S(1)} %get-tuple-element.4, f32[2,640,128]{2,1,0:T(8,128)S(1)} %get-tuple-element.5), kind=kLoop, calls=%fused_computation | loop fusion | bytes 2621440 | tf_op jit(solution)/shard_map/reshape | solution.py:639

commit v7 on v6

--- a/solution.py
+++ b/solution.py
@@ -171,9 +171,14 @@
             device_id=at(d), device_id_type=MESH)
 
     def store_field(f, j, parts):
+        store_chunk(f, j, parts)
+        store_ends(f, j, parts)
+
+    def store_chunk(f, j, parts):
         for t in range(TILES):
             wbuf[f, j + 1, :, t] = parts[t]
 
+    def store_ends(f, j, parts):
         @pl.when(j == 0)
         def _():
             for t in range(TILES):
@@ -409,9 +414,12 @@
     turn(fs, hbuf)
 
     def second(j, late):
+        def fetch():
+            await_corners(0, j)
+            return corner_values(0, j, 0)
+
         await_rims(0, j)
-        await_corners(0, j)
-        spreads = spread(COUPLING, 0, j, corner_values(0, j, 0))
+        spreads = spread(COUPLING, 0, j, fetch if late else fetch())
         couplings = [wbuf[COUPLING, j + 1, :, t] for t in range(TILES)]
         diagonals = [gbuf[j, :, t] + couplings[t] * spreads[t] for t in range(TILES)]
         ratios = [couplings[t] / diagonals[t] for t in range(TILES)]
@@ -443,12 +451,15 @@
         def step(j, late):
             if not late:
                 await_rims(k, j)
+            held = []
+
+            def fetch():
+                await_corners(k, j)
+                held.extend(corner_values(k, j, 0))
+                return held
+
             if place == "first":
-                await_corners(k, j)
-                corners = corner_values(k, j, 0)
-                scales = corner_values(k, j, 64)
-                for p in range(2):
-                    ecbuf[j, p] = scales[p]
+                corners = fetch if late else fetch()
             else:
                 ahead = jnp.bool_(True) if place == "last" else k > 2
                 if late:
@@ -457,7 +468,8 @@
                     await_half(k - 1, 1, jnp.logical_and(ahead, j == HALF))
                 corners = next_corners(k, j)
             if late:
-                store_corners(k, j, corners)
+                if place != "first":
+                    store_corners(k, j, corners)
                 await_rims(k, j)
             spreads = spread(k, k, j, corners)
             applied = [ebuf[j, :, t] * spreads[t] for t in range(TILES)]
@@ -469,12 +481,22 @@
                 return
             if not late:
                 rest(j - 1)
+            store_chunk(k + 1, j, parts)
+            if not late:
+                store_ends(k + 1, j, parts)
+            send_rims(k + 1, j, ALONG_X)
+            if late:
+                store_ends(k + 1, j, parts)
             for t in range(TILES):
                 abuf[:, t] = applied[t]
-            store_field(k + 1, j, parts)
-            send_rims(k + 1, j, ALONG_X)
+            if place == "first":
+                scales = corner_values(k, j, 64)
+                for p in range(2):
+                    ecbuf[j, p] = scales[p]
+                store_corners(k, j, held)
+            elif not late:
+                store_corners(k, j, corners)
             if not late:
-                store_corners(k, j, corners)
                 send_rims(k + 1, j - 1, BESIDE[:2])
                 send_half(k + 1, 0, jnp.logical_and(j == HALF, sends_corners))
 

time: 53.5 us -> 53.4 us (level)
  no operation moved by 1% of the time
where the time goes in v7:
time: 53.4 us; the launch traced here: 53.3 us
  Pallas kernels  51.5 us (96%)
  local copies, waits for them, and re-layouts  1.16 us (2%)
  between operations  0.64 us (1%)
    pallas_call x1, Pallas kernels, on_device(): pl.pallas_call(functools.partial(kernel, nx, nz), out_shape=(out, out), i...  51.5 us
    reshape x1, local copies, waits for them, and re-layouts, on_device(): v.reshape(TILES, LAYERS, ROWS, LANES).transpose(1, 2, 0, 3)  1.16 us

profile of v7, /device:TPU:2, one launch (start us, length us, event | category | flops | bytes accessed | tf_op | source)
XLA Modules:
  0.0 53.3 jit_solution(13894172725035686995)
XLA Ops:
  0.6 51.5 %coupled_solve.1 = (f32[2,640,128]{2,1,0:T(8,128)S(1)}, f32[2,640,128]{2,1,0:T(8,128)S(1)}) custom-call(f32[640,256]{1,0:T(8,128)} %bitcast.17, bf16[8,80,256]{2,1,0:T(8,128)(2,1)} %bitcast.18, bf16[640,256]{1,0:T(8,128)(2,1)} %bitcast.19, s32[8,256]{1,0:T(8,128)} %ice_mask.1, s32[8,256]{1,0:T(8,128)} %grounded.1), custom_call_target="tpu_custom_call" | custom-call | tf_op jit(solution)/shard_map/coupled_solve/pallas_call | solution.py:615
  52.2 1.2 %copy_bitcast_fusion = (f32[1,80,8,256]{3,2,1,0:T(8,128)}, f32[1,80,8,256]{3,2,1,0:T(8,128)}) fusion(f32[2,640,128]{2,1,0:T(8,128)S(1)} %get-tuple-element.4, f32[2,640,128]{2,1,0:T(8,128)S(1)} %get-tuple-element.5), kind=kLoop, calls=%fused_computation | loop fusion | bytes 2621440 | tf_op jit(solution)/shard_map/reshape | solution.py:661
